TPU v7x, 8 devices: a whole 2x2x1 slice. The times are simulated.
8 devices in a mesh: dp: 1 (over z), tp: 2 (over y), cp: 4 (over x, core).
Axes of the slice: x: 2, y: 2, z: 1, core: 2. Of those that a mesh axis runs over, the one named last changes fastest.
Arguments:
- x_in: bfloat16 [4096, 896], P(('dp', 'cp', 'tp'))
- w_query: bfloat16 [896, 14, 64], P(None, 'tp')
- w_key: bfloat16 [896, 2, 64], P(None, 'tp')
- w_value: bfloat16 [896, 2, 64], P(None, 'tp')
- w_out: bfloat16 [14, 64, 896], P('tp')
- d_out: bfloat16 [4096, 896], P(('dp', 'cp', 'tp'))
Outputs:
- output 1: bfloat16 [4096, 896], P(('dp', 'cp', 'tp'))
- output 2: bfloat16 [4096, 896], P(('dp', 'cp', 'tp'))
- output 3: bfloat16 [4, 896, 14, 64], P(('dp', 'cp'), None, 'tp')
- output 4: bfloat16 [4, 896, 2, 64], P(('dp', 'cp'), None, 'tp')
- output 5: bfloat16 [4, 896, 2, 64], P(('dp', 'cp'), None, 'tp')
- output 6: bfloat16 [4, 14, 64, 896], P(('dp', 'cp'), 'tp')
All inputs are finite; a program needn't handle non-finite values.
Results may differ from a plain program's by a relative error of at most 0.0103152.
Values are sent between devices in bfloat16 or wider.
A program may use at most 1 GiB of HBM per device.

v0:
```python
import functools
import math

import jax
import jax.numpy as jnp
from jax import lax
from jax.experimental import pallas as pl
from jax.experimental.pallas import tpu as pltpu
from jax.sharding import PartitionSpec as P

ROW_SPEC = P(("dp", "cp", "tp"), None)
HEAD_SPEC = P(None, "tp", None)
OUT_W_SPEC = P("tp", None, None)
GRAD_SPEC = P(("dp", "cp"), None, "tp", None)
GRAD_OUT_SPEC = P(("dp", "cp"), "tp", None, None)
F32 = jnp.float32
BF16 = jnp.bfloat16
NT = (((1,), (1,)), ((), ()))
TN = (((0,), (0,)), ((), ()))
VMEM = pl.BlockSpec(memory_space=pltpu.VMEM)
ANY = pl.BlockSpec(memory_space=pl.ANY)
VMEM_LIMIT = 64 * 1024 * 1024
N_COPIES = 22


def dot(a, b):
    return jnp.dot(a, b, preferred_element_type=F32)


def dot_nt(a, b):
    return lax.dot_general(a, b, NT, preferred_element_type=F32)


def dot_tn(a, b):
    return lax.dot_general(a, b, TN, preferred_element_type=F32)


def far_units(rank, half, shards):
    units = []
    for d in range(1, shards):
        early = (rank + shards - d) // shards
        slot = early * half + (1 - early) * (1 - half)
        units += [(slot, 2 * d + half, early), (1 - half, 2 * d + slot, 0)]
    return units


def diag_mask(size):
    return lax.broadcasted_iota(jnp.int32, (size, size), 1) >= lax.broadcasted_iota(jnp.int32, (size, size), 0)


def pick(first, pair):
    if isinstance(first, int):
        return pair[1 - first]
    return jnp.where(first == 1, pair[0], pair[1])


def add_to(pair, first, value):
    if isinstance(first, int):
        pair[1 - first] = pair[1 - first] + value
    else:
        pair[0] = pair[0] + jnp.where(first == 1, value, 0.0)
        pair[1] = pair[1] + jnp.where(first == 1, 0.0, value)


def transpose_bf16(x):
    return x.astype(F32).T.astype(BF16)


def kernel(shards, n_heads, hd, c_scale, scale,
           x_hbm, dy_hbm, wq_hbm, wk_hbm, wv_hbm, wo_hbm,
           y_ref, dx_ref, gq_ref, gk_ref, gv_ref, go_ref,
           x_s, xp, dy_s, dyp, wq, wk, wv, wo, wqp, wkp, wvp, wop,
           q_s, do_s, o_s, og, dq_s, dqg, kvt, k_s, v_s, acc, m_s, l_s, s_s, dkv, rcv, dkvb, dkvg,
           send, recv, local):
    rank = lax.axis_index("cp")
    half = lax.axis_index("tp")
    core = rank % 2
    cols = q_s.shape[-1]
    hw = n_heads * hd
    groups = cols // 8
    peer = {"tp": 1 - half}
    partner = {"cp": rank + 1 - 2 * core}

    def at_cp(i):
        return {"cp": i % shards}

    def copy(i, src, dst, device):
        return pltpu.make_async_remote_copy(src_ref=src, dst_ref=dst, send_sem=send.at[i], recv_sem=recv.at[i],
                                            device_id=device, device_id_type=pl.DeviceIdType.MESH)

    loads = [pltpu.make_async_copy(src, dst, local.at[i]) for i, (src, dst) in enumerate(
        [(x_hbm, x_s), (wk_hbm, wk), (wv_hbm, wv), (wq_hbm, wq), (wo_hbm, wo), (dy_hbm, dy_s)])]
    for c in loads:
        c.start()
    barrier = pltpu.get_barrier_semaphore()
    pl.semaphore_signal(barrier, inc=1, device_id=peer, device_id_type=pl.DeviceIdType.MESH)
    for d in range(1, shards):
        pl.semaphore_signal(barrier, inc=1, device_id=at_cp(rank + d), device_id_type=pl.DeviceIdType.MESH)
    pl.semaphore_wait(barrier, shards)

    c_x = copy(0, x_hbm, xp, peer)
    c_dy = copy(1, dy_hbm, dyp, peer)
    c_w = [copy(2 + i, src.at[core], dst.at[core], peer)
           for i, (src, dst) in enumerate([(wo_hbm, wop), (wq_hbm, wqp), (wk_hbm, wkp), (wv_hbm, wvp)])]
    c_relay = [copy(6 + i, dst.at[core], dst.at[core], partner) for i, dst in enumerate([wop, wqp, wkp, wvp])]
    c_x.start()
    c_dy.start()
    for c in c_w:
        c.start()

    def flat(ref):
        return ref[...].reshape(ref.shape[0] * ref.shape[1], ref.shape[2])

    def send_kv(slot):
        cs = [copy(10 + 3 * slot + d - 1, kvt.at[slot], kvt.at[2 * d + slot], at_cp(rank + d)) for d in range(1, shards)]
        for c in cs:
            c.start()
        return cs

    def keys_ready(tile):
        k_s[tile] = transpose_bf16(kvt[tile, :hd, :])
        v_s[tile] = transpose_bf16(kvt[tile, hd:, :])

    for c in loads[:3]:
        c.wait()
    kvt[0, :hd, :] = dot_nt(flat(wk), x_s[...]).astype(BF16)
    kvt[0, hd:, :] = dot_nt(flat(wv), x_s[...]).astype(BF16)
    c_kv = send_kv(0)
    loads[3].wait()
    q_s[0] = dot_nt(flat(wq), x_s[...]).astype(BF16).reshape(n_heads, hd, cols)
    loads[4].wait()
    loads[5].wait()
    do_s[0] = dot_nt(flat(wo), dy_s[...]).astype(BF16).reshape(n_heads, hd, cols)
    keys_ready(0)
    c_x.wait_recv()
    kvt[1, :hd, :] = dot_nt(flat(wk), xp[...]).astype(BF16)
    kvt[1, hd:, :] = dot_nt(flat(wv), xp[...]).astype(BF16)
    c_kv += send_kv(1)
    q_s[1] = dot_nt(flat(wq), xp[...]).astype(BF16).reshape(n_heads, hd, cols)
    keys_ready(1)

    near = [(half, half, 1, True), (1 - half, half, 0, False), (1 - half, 1 - half, 0, True)]
    far = [u + (False,) for u in far_units(rank, half, shards)]
    slots = (half, 1 - half)

    def forward(units, h, is_near):
        maxes = [None, None]
        for u, (qi, kt, first, diag) in enumerate(units):
            s = dot(k_s[kt], q_s[qi, h])
            if diag:
                s = jnp.where(diag_mask(cols), s, -jnp.inf)
            s_s[u] = s
            mx = jnp.max(s.reshape(groups, 8, cols), axis=0)
            for g in (0, 1):
                if isinstance(first, int):
                    if first == g:
                        continue
                    val = mx
                else:
                    val = jnp.where(first == 1 - g, mx, -jnp.inf)
                maxes[g] = val if maxes[g] is None else jnp.maximum(maxes[g], val)
        m = [jnp.max(v, axis=0, keepdims=True) * c_scale for v in maxes]
        if is_near:
            l = [jnp.zeros((8, cols), F32), jnp.zeros((8, cols), F32)]
            o = [jnp.zeros((hd, cols), F32), jnp.zeros((hd, cols), F32)]
        else:
            old = [m_s[slots[g], h] for g in (0, 1)]
            m = [jnp.maximum(a, b) for a, b in zip(m, old)]
            fix = [jnp.exp2(a - b) for a, b in zip(old, m)]
            l = [l_s[slots[g], h] * fix[g] for g in (0, 1)]
            o = [acc[slots[g], h] * fix[g] for g in (0, 1)]
        for u, (qi, kt, first, diag) in enumerate(units):
            p = jnp.exp2(s_s[u] * c_scale - pick(first, m))
            add_to(l, first, jnp.sum(p.reshape(groups, 8, cols), axis=0))
            add_to(o, first, dot(kvt[kt, hd:, :], p.astype(BF16)))
        for g in (0, 1):
            if is_near:
                m_s[slots[g], h] = m[g]
                l_s[slots[g], h] = l[g]
                acc[slots[g], h] = o[g]
            else:
                l_row = jnp.sum(l[g], axis=0, keepdims=True)
                o_s[slots[g], h] = (o[g] / l_row).astype(BF16)
                m_s[slots[g], h] = m[g] + jnp.log2(l_row)

    def near_fwd(h, _):
        forward(near, h, True)
        return 0

    def far_fwd(h, _):
        forward(far, h, False)
        copy(20, o_s.at[1, h], og.at[h], peer).start()
        return 0

    lax.fori_loop(0, n_heads, near_fwd, 0)
    for i, c in enumerate(c_kv):
        c.wait_recv()
    for tile in range(2, 2 * shards):
        keys_ready(tile)
    lax.fori_loop(0, n_heads, far_fwd, 0)
    for c in c_w:
        c.wait_recv()
    for c in c_relay:
        c.start()
    c_dy.wait_recv()
    do_s[1] = dot_nt(flat(wo), dyp[...]).astype(BF16).reshape(n_heads, hd, cols)
    dkv[...] = jnp.zeros_like(dkv)

    def backward(units, h):
        delta = [jnp.sum(do_s[s, h].astype(F32) * o_s[s, h].astype(F32), axis=0, keepdims=True) for s in slots]
        lse = [m_s[s, h] for s in slots]
        dq = [jnp.zeros((hd, cols), F32), jnp.zeros((hd, cols), F32)]
        for qi, kt, first, diag in units:
            q, do = q_s[qi, h], do_s[qi, h]
            p = jnp.exp2(dot(k_s[kt], q) * c_scale - pick(first, lse))
            if diag:
                p = jnp.where(diag_mask(cols), p, 0.0)
            ds = (p * (dot(v_s[kt], do) - pick(first, delta))).astype(BF16)
            dkv[kt, hd:, :] += dot_nt(do, p.astype(BF16))
            dkv[kt, :hd, :] += dot_nt(q, ds)
            add_to(dq, first, dot(kvt[kt, :hd, :], ds))
        return dq

    def far_bwd(h, _):
        dq = backward(far, h)
        for g in (0, 1):
            acc[slots[g], h] = dq[g]
        return 0

    def near_bwd(h, _):
        dq = backward(near, h)
        for g in (0, 1):
            dq_s[slots[g], h] = ((dq[g] + acc[slots[g], h]) * scale).astype(BF16)
        copy(21, dq_s.at[1, h], dqg.at[h], peer).start()
        return 0

    lax.fori_loop(0, n_heads, far_bwd, 0)
    c_dkv = [copy(16 + d - 1, dkv.at[pl.ds(2 * d, 2)], rcv.at[d - 1], at_cp(rank + shards - d)) for d in range(1, shards)]
    for c in c_dkv:
        c.start()
    lax.fori_loop(0, n_heads, near_bwd, 0)

    for c in c_relay:
        c.wait_recv()
    c_o = copy(20, o_s.at[1], og, peer)
    c_o.wait_recv()
    rows = 128
    for i in range(cols // rows):
        part = slice(i * rows, (i + 1) * rows)
        y = dot_tn(o_s[0, :, :, part].reshape(hw, rows), flat(wo)) + dot_tn(og[:, :, part].reshape(hw, rows), flat(wop))
        y_ref[part, :] = y.astype(BF16)
    for h in range(n_heads):
        go_ref[h] = (dot(o_s[0, h], dy_s[...]) + dot(o_s[1, h], dyp[...])).astype(BF16)
        gq_ref[h] = (dot(dq_s[0, h], x_s[...]) + dot(dq_s[1, h], xp[...])).astype(BF16)

    for c in c_dkv:
        c.wait_recv()
    for slot in (1, 0):
        total = dkv[slot] + rcv[0, slot] + rcv[1, slot] + rcv[2, slot]
        dkvb[slot, :hd, :] = (total[:hd, :] * scale).astype(BF16)
        dkvb[slot, hd:, :] = total[hd:, :].astype(BF16)
    c_last = copy(19, dkvb.at[1], dkvg, peer)
    c_last.start()
    gkv = dot(dkvb[0], x_s[...]) + dot(dkvb[1], xp[...])
    gk_ref[...] = gkv[:hd, :].astype(BF16)
    gv_ref[...] = gkv[hd:, :].astype(BF16)
    c_dq = copy(21, dq_s.at[1], dqg, peer)
    c_dq.wait_recv()
    c_last.wait_recv()
    for i in range(cols // rows):
        part = slice(i * rows, (i + 1) * rows)
        dx = dot_tn(dq_s[0, :, :, part].reshape(hw, rows), flat(wq)) + dot_tn(dqg[:, :, part].reshape(hw, rows), flat(wqp))
        dx += dot_tn(dkvb[0, :hd, part], flat(wk)) + dot_tn(dkvb[0, hd:, part], flat(wv))
        dx += dot_tn(dkvg[:hd, part], flat(wkp)) + dot_tn(dkvg[hd:, part], flat(wvp))
        dx_ref[part, :] = dx.astype(BF16)
    for c in [c_x, c_dy, c_o, c_dq, c_last] + c_w + c_relay + c_kv + c_dkv:
        c.wait_send()


def solution(mesh):
    shards = mesh.shape["cp"]

    def device_fn(x_own, w_query, w_key, w_value, w_out, dy_own):
        model, n_heads, hd = w_query.shape
        cols = x_own.shape[0]
        hw = n_heads * hd
        scale = hd ** -0.5
        wq = w_query.transpose(1, 2, 0).reshape(2, hw // 2, model)
        wk = w_key.transpose(1, 2, 0).reshape(2, hd // 2, model)
        wv = w_value.transpose(1, 2, 0).reshape(2, hd // 2, model)
        wo = w_out.reshape(2, hw // 2, model)
        per_head = (2, n_heads, hd, cols)
        b = lambda *s: pltpu.VMEM(s, BF16)
        f = lambda *s: pltpu.VMEM(s, F32)
        area = n_heads * 9 * cols * cols
        y, dx, gq, gk, gv, go = pl.pallas_call(
            functools.partial(kernel, shards, n_heads, hd, scale * math.log2(math.e), scale),
            out_shape=(jax.ShapeDtypeStruct((cols, model), BF16), jax.ShapeDtypeStruct((cols, model), BF16),
                       jax.ShapeDtypeStruct((n_heads, hd, model), BF16), jax.ShapeDtypeStruct((hd, model), BF16),
                       jax.ShapeDtypeStruct((hd, model), BF16), jax.ShapeDtypeStruct((n_heads, hd, model), BF16)),
            in_specs=[ANY] * 6,
            out_specs=(VMEM,) * 6,
            scratch_shapes=[b(cols, model)] * 4 + [b(2, hw // 2, model), b(2, hd // 2, model), b(2, hd // 2, model), b(2, hw // 2, model)] * 2
            + [b(*per_head), b(*per_head), b(*per_head), b(*per_head[1:]), b(*per_head), b(*per_head[1:]),
               b(2 * shards, 2 * hd, cols), b(2 * shards, cols, hd), b(2 * shards, cols, hd), f(*per_head),
               f(2, n_heads, 1, cols), f(2, n_heads, 8, cols), f(6, cols, cols), f(2 * shards, 2 * hd, cols),
               f(shards - 1, 2, 2 * hd, cols), b(2, 2 * hd, cols), b(2 * hd, cols),
               pltpu.SemaphoreType.DMA((N_COPIES,)), pltpu.SemaphoreType.DMA((N_COPIES,)), pltpu.SemaphoreType.DMA((6,))],
            compiler_params=pltpu.CompilerParams(vmem_limit_bytes=VMEM_LIMIT, collective_id=0, has_side_effects=True),
            cost_estimate=pl.CostEstimate(flops=area * 7 * 2 * hd, bytes_accessed=16 << 20, transcendentals=2 * area),
            name="attention",
        )(x_own, dy_own, wq, wk, wv, wo)
        back = lambda g, n: g.reshape(n, hd, model).transpose(2, 0, 1)[None]
        return y, dx, back(gq, n_heads), back(gk, 1), back(gv, 1), go[None]

    return jax.shard_map(device_fn, mesh=mesh,
                         in_specs=(ROW_SPEC, HEAD_SPEC, HEAD_SPEC, HEAD_SPEC, OUT_W_SPEC, ROW_SPEC),
                         out_specs=(ROW_SPEC, ROW_SPEC, GRAD_SPEC, GRAD_SPEC, GRAD_SPEC, GRAD_OUT_SPEC),
                         check_vma=False)
```

profile of v0, /device:TPU:0, one launch (start us, length us, event | category | flops | bytes accessed | tf_op | source)
XLA Modules:
  0.0 132.4 jit_solution(1309422334370887482)
XLA Ops:
  0.6 124.5 %attention.1 = (bf16[512,896]{1,0:T(8,128)(2,1)}, bf16[512,896]{1,0:T(8,128)(2,1)}, bf16[7,64,896]{2,1,0:T(8,128)(2,1)}, bf16[64,896]{1,0:T(8,128)(2,1)}, bf16[6...) custom-call(bf16[512,896]{1,0:T(8,128)(2,1)} %x_hbm.1, bf16[512,896]{1,0:T(8,128)(2,1)} %dy_hbm.1, ...), custom_call_target="tpu_custom_call" | custom-call | flops 14797504512 | bytes 16777216 | tf_op jit(solution)/shard_map/attention/pallas_call | solution.py:296
  125.2 0.0 copy-start
  125.2 2.3 %copy.18 = bf16[512,896]{1,0:T(8,128)(2,1)} copy(bf16[512,896]{1,0:T(8,128)(2,1)} %get-tuple-element.24) | data formatting | bytes 1835008
  127.4 0.0 copy-done
  127.4 0.0 copy-start.2
  127.4 0.9 copy.19
  128.4 0.5 copy-done.2
  128.9 0.0 copy-start.4
  128.9 0.0 copy-start.1
  128.9 0.9 copy.20
  129.8 0.1 copy-done.4
  129.9 0.0 copy-start.3
  129.9 0.6 copy.21
  130.5 0.3 copy-done.3
  130.8 0.6 copy.22
  131.5 0.0 copy-done.1
  131.5 0.9 copy.23
Async XLA Ops:
  125.2 2.3 %copy-start = (bf16[512,896]{1,0:T(8,128)(2,1)S(1)}, bf16[512,896]{1,0:T(8,128)(2,1)}, u32[]{:S(2)}) copy-start(bf16[512,896]{1,0:T(8,128)(2,1)} %get-tuple-element.25) | copy-start | bytes 2752516
  127.4 1.5 %copy-start.2 = (bf16[7,64,896]{2,1,0:T(8,128)(2,1)S(1)}, bf16[7,64,896]{2,1,0:T(8,128)(2,1)}, u32[]{:S(2)}) copy-start(bf16[7,64,896]{2,1,0:T(8,128)(2,1)} %get-tuple-element.14) | copy-start | bytes 2408452
  128.9 1.0 copy-start.4
  128.9 2.6 %copy-start.1 = (bf16[7,64,896]{2,1,0:T(8,128)(2,1)S(1)}, bf16[7,64,896]{2,1,0:T(8,128)(2,1)}, u32[]{:S(2)}) copy-start(bf16[7,64,896]{2,1,0:T(8,128)(2,1)} %get-tuple-element.17) | copy-start | bytes 2408452
  129.9 0.9 copy-start.3
where the time goes:
time: 133 us; the launch traced here: 132 us
  Pallas kernels  125 us (94%)
  local copies, waits for them, and re-layouts  7.19 us (5%)
    pallas_call x1, Pallas kernels, device_fn(): pl.pallas_call(functools.partial(kernel, shards, n_heads, hd, scale * mat...  125 us
    unnamed x16, local copies, waits for them, and re-layouts  7.19 us

commit v1 on v0

--- a/solution.py
+++ b/solution.py
@@ -70,14 +70,13 @@
            x_hbm, dy_hbm, wq_hbm, wk_hbm, wv_hbm, wo_hbm,
            y_ref, dx_ref, gq_ref, gk_ref, gv_ref, go_ref,
            x_s, xp, dy_s, dyp, wq, wk, wv, wo, wqp, wkp, wvp, wop,
-           q_s, do_s, o_s, og, dq_s, dqg, kvt, k_s, v_s, acc, m_s, l_s, s_s, dkv, rcv, dkvb, dkvg,
+           q_s, do_s, o_s, og, dq_s, dqg, kvt, k_s, v_s, acc, m_s, l_s, d_s, max_s, s_s, pb, db, dkv, rcv, dkvb, dkvg,
            send, recv, local):
     rank = lax.axis_index("cp")
     half = lax.axis_index("tp")
     core = rank % 2
     cols = q_s.shape[-1]
     hw = n_heads * hd
-    groups = cols // 8
     peer = {"tp": 1 - half}
     partner = {"cp": rank + 1 - 2 * core}
 
@@ -142,103 +141,223 @@
     near = [(half, half, 1, True), (1 - half, half, 0, False), (1 - half, 1 - half, 0, True)]
     far = [u + (False,) for u in far_units(rank, half, shards)]
     slots = (half, 1 - half)
-
-    def forward(units, h, is_near):
-        maxes = [None, None]
-        for u, (qi, kt, first, diag) in enumerate(units):
-            s = dot(k_s[kt], q_s[qi, h])
-            if diag:
-                s = jnp.where(diag_mask(cols), s, -jnp.inf)
-            s_s[u] = s
-            mx = jnp.max(s.reshape(groups, 8, cols), axis=0)
-            for g in (0, 1):
+    part = cols // 2
+    triangle = diag_mask(part)
+
+    def spans(diag, c):
+        return slice(c * part, (c + 1) * part), slice(c * part, cols) if diag else slice(0, cols)
+
+    def masked(x, diag, fill):
+        if not diag:
+            return x
+        left = jnp.where(triangle, x[:, :part], fill)
+        return left if x.shape[1] == part else jnp.concatenate([left, x[:, part:]], axis=1)
+
+    def widen(x, fill):
+        if x.shape[1] == cols:
+            return x
+        return jnp.concatenate([jnp.full((x.shape[0], cols - x.shape[1]), fill, x.dtype), x], axis=1)
+
+    def interleave(first_list, second_list):
+        i = j = 0
+        while i < len(first_list) or j < len(second_list):
+            if j >= len(second_list) or (i < len(first_list) and i * len(second_list) <= j * len(first_list)):
+                first_list[i]()
+                i += 1
+            else:
+                second_list[j]()
+                j += 1
+
+    def score_steps(units, base, h, maxes):
+        def step(u, c):
+            qi, kt, first, diag = units[u]
+            r, q = spans(diag, c)
+            s = masked(dot(k_s[kt, r], q_s[qi, h, :, q]), diag, -jnp.inf)
+            s_s[base + u, r, q] = s
+            mx = widen(jnp.max(s.reshape(part // 8, 8, s.shape[1]), axis=0), -jnp.inf)
+            maxes[u] = mx if c == 0 else jnp.maximum(maxes[u], mx)
+        return [functools.partial(step, u, c) for u in range(len(units)) for c in (0, 1)]
+
+    def score_max(units, maxes):
+        for g in (0, 1):
+            best = None
+            for u, (_, _, first, _) in enumerate(units):
                 if isinstance(first, int):
                     if first == g:
                         continue
-                    val = mx
+                    val = maxes[u]
                 else:
-                    val = jnp.where(first == 1 - g, mx, -jnp.inf)
-                maxes[g] = val if maxes[g] is None else jnp.maximum(maxes[g], val)
-        m = [jnp.max(v, axis=0, keepdims=True) * c_scale for v in maxes]
+                    val = jnp.where(first == 1 - g, maxes[u], -jnp.inf)
+                best = val if best is None else jnp.maximum(best, val)
+            max_s[g] = jnp.max(best, axis=0, keepdims=True) * c_scale
+
+    def attend_steps(units, base, h, is_near):
+        m = [max_s[0], max_s[1]]
         if is_near:
             l = [jnp.zeros((8, cols), F32), jnp.zeros((8, cols), F32)]
             o = [jnp.zeros((hd, cols), F32), jnp.zeros((hd, cols), F32)]
         else:
             old = [m_s[slots[g], h] for g in (0, 1)]
-            m = [jnp.maximum(a, b) for a, b in zip(m, old)]
-            fix = [jnp.exp2(a - b) for a, b in zip(old, m)]
+            m = [jnp.maximum(x, y) for x, y in zip(m, old)]
+            fix = [jnp.exp2(x - y) for x, y in zip(old, m)]
             l = [l_s[slots[g], h] * fix[g] for g in (0, 1)]
             o = [acc[slots[g], h] * fix[g] for g in (0, 1)]
-        for u, (qi, kt, first, diag) in enumerate(units):
-            p = jnp.exp2(s_s[u] * c_scale - pick(first, m))
-            add_to(l, first, jnp.sum(p.reshape(groups, 8, cols), axis=0))
-            add_to(o, first, dot(kvt[kt, hd:, :], p.astype(BF16)))
-        for g in (0, 1):
-            if is_near:
-                m_s[slots[g], h] = m[g]
-                l_s[slots[g], h] = l[g]
-                acc[slots[g], h] = o[g]
+        sums = {}
+
+        def step(u, c):
+            qi, kt, first, diag = units[u]
+            r, q = spans(diag, c)
+            p = jnp.exp2(s_s[base + u, r, q] * c_scale - pick(first, m)[:, q])
+            l_u = widen(jnp.sum(p.reshape(part // 8, 8, p.shape[1]), axis=0), 0.0)
+            o_u = widen(dot(kvt[kt, hd:, r], p.astype(BF16)), 0.0)
+            if c == 0:
+                sums[u] = (l_u, o_u)
             else:
-                l_row = jnp.sum(l[g], axis=0, keepdims=True)
-                o_s[slots[g], h] = (o[g] / l_row).astype(BF16)
-                m_s[slots[g], h] = m[g] + jnp.log2(l_row)
+                add_to(l, first, sums[u][0] + l_u)
+                add_to(o, first, sums[u][1] + o_u)
+
+        def finish():
+            for g in (0, 1):
+                if is_near:
+                    m_s[slots[g], h] = m[g]
+                    l_s[slots[g], h] = l[g]
+                    acc[slots[g], h] = o[g]
+                else:
+                    l_row = jnp.sum(l[g], axis=0, keepdims=True)
+                    o_s[slots[g], h] = (o[g] / l_row).astype(BF16)
+                    m_s[slots[g], h] = m[g] + jnp.log2(l_row)
+
+        return [functools.partial(step, u, c) for u in range(len(units)) for c in (0, 1)], finish
+
+    def forward(units, base, h, is_near, nxt):
+        steps, finish = attend_steps(units, base, h, is_near)
+        maxes = {}
+        following = score_steps(*nxt, maxes) if nxt else []
+        interleave(steps, following)
+        finish()
+        if nxt:
+            score_max(nxt[0], maxes)
+
+    def send_o(h):
+        copy(20, o_s.at[1, h], og.at[h], peer).start()
 
     def near_fwd(h, _):
-        forward(near, h, True)
+        forward(near, 6, h, True, (near, 6, h + 1))
         return 0
 
     def far_fwd(h, _):
-        forward(far, h, False)
-        copy(20, o_s.at[1, h], og.at[h], peer).start()
+        forward(far, 0, h, False, (far, 0, h + 1))
+        send_o(h)
         return 0
 
-    lax.fori_loop(0, n_heads, near_fwd, 0)
+    last = n_heads - 1
+    maxes = {}
+    for step in score_steps(near, 6, 0, maxes):
+        step()
+    score_max(near, maxes)
+    lax.fori_loop(0, last, near_fwd, 0)
     for i, c in enumerate(c_kv):
         c.wait_recv()
     for tile in range(2, 2 * shards):
         keys_ready(tile)
-    lax.fori_loop(0, n_heads, far_fwd, 0)
+    forward(near, 6, last, True, (far, 0, 0))
+    lax.fori_loop(0, last, far_fwd, 0)
     for c in c_w:
         c.wait_recv()
     for c in c_relay:
         c.start()
     c_dy.wait_recv()
     do_s[1] = dot_nt(flat(wo), dyp[...]).astype(BF16).reshape(n_heads, hd, cols)
+    forward(far, 0, last, False, None)
+    send_o(last)
     dkv[...] = jnp.zeros_like(dkv)
 
-    def backward(units, h):
-        delta = [jnp.sum(do_s[s, h].astype(F32) * o_s[s, h].astype(F32), axis=0, keepdims=True) for s in slots]
-        lse = [m_s[s, h] for s in slots]
+    def row_dots(h, _):
+        for s in (0, 1):
+            d_s[s, h] = jnp.sum(do_s[s, h].astype(F32) * o_s[s, h].astype(F32), axis=0, keepdims=True)
+        return 0
+
+    lax.fori_loop(0, n_heads, row_dots, 0)
+
+    def prob_steps(units, bufs, h, which):
+        def step(u, c):
+            qi, kt, first, diag = units[u]
+            r, q = spans(diag, c)
+            buf = bufs[u % len(bufs)]
+            p = jnp.exp2(dot(k_s[kt, r], q_s[qi, h, :, q]) * c_scale - m_s[qi, h, :, q])
+            p = masked(p, diag, 0.0)
+            pb[buf, r, q] = p.astype(BF16)
+            db[buf, r, q] = (p * (dot(v_s[kt, r], do_s[qi, h, :, q]) - d_s[qi, h, :, q])).astype(BF16)
+        return [functools.partial(step, u, c) for u in which for c in (0, 1)]
+
+    def grad_steps(units, bufs, h, u, dq):
+        qi, kt, first, diag = units[u]
+        buf = bufs[u % len(bufs)]
+        kept = {}
+
+        def over_queries(name, src, lhs, rows, c):
+            q = slice(c * part, (c + 1) * part)
+            keys = slice(0, part) if diag and c == 0 else slice(0, cols)
+            val = dot_nt(lhs[qi, h, :, q], src[buf, keys, q])
+            if c == 0 and not diag:
+                kept[name] = val
+            elif diag:
+                dkv[kt, rows, keys] += val
+            else:
+                dkv[kt, rows, :] += kept[name] + val
+
+        def over_keys(c):
+            r, q = spans(diag, c)
+            val = widen(dot(kvt[kt, :hd, r], db[buf, r, q]), 0.0)
+            if c == 0:
+                kept["q"] = val
+            else:
+                add_to(dq, first, kept["q"] + val)
+
+        return ([functools.partial(over_queries, "v", pb, do_s, slice(hd, 2 * hd), c) for c in (0, 1)]
+                + [functools.partial(over_queries, "k", db, q_s, slice(0, hd), c) for c in (0, 1)]
+                + [functools.partial(over_keys, c) for c in (0, 1)])
+
+    def backward(units, bufs, h, nxt):
         dq = [jnp.zeros((hd, cols), F32), jnp.zeros((hd, cols), F32)]
-        for qi, kt, first, diag in units:
-            q, do = q_s[qi, h], do_s[qi, h]
-            p = jnp.exp2(dot(k_s[kt], q) * c_scale - pick(first, lse))
-            if diag:
-                p = jnp.where(diag_mask(cols), p, 0.0)
-            ds = (p * (dot(v_s[kt], do) - pick(first, delta))).astype(BF16)
-            dkv[kt, hd:, :] += dot_nt(do, p.astype(BF16))
-            dkv[kt, :hd, :] += dot_nt(q, ds)
-            add_to(dq, first, dot(kvt[kt, :hd, :], ds))
+        for u in range(len(units)):
+            if u + 1 < len(units):
+                ahead = prob_steps(units, bufs, h, [u + 1])
+            else:
+                ahead = prob_steps(*nxt, [0]) if nxt else []
+            interleave(ahead, grad_steps(units, bufs, h, u, dq))
         return dq
 
-    def far_bwd(h, _):
-        dq = backward(far, h)
+    near_bufs, far_bufs = (0, 1, 2), (3, 4)
+
+    def far_bwd(h, nxt):
+        dq = backward(far, far_bufs, h, nxt)
         for g in (0, 1):
             acc[slots[g], h] = dq[g]
-        return 0
-
-    def near_bwd(h, _):
-        dq = backward(near, h)
+
+    def near_bwd(h, nxt):
+        dq = backward(near, near_bufs, h, nxt)
         for g in (0, 1):
             dq_s[slots[g], h] = ((dq[g] + acc[slots[g], h]) * scale).astype(BF16)
         copy(21, dq_s.at[1, h], dqg.at[h], peer).start()
+
+    def far_loop(h, _):
+        far_bwd(h, (far, far_bufs, h + 1))
         return 0
 
-    lax.fori_loop(0, n_heads, far_bwd, 0)
+    def near_loop(h, _):
+        near_bwd(h, (near, near_bufs, h + 1))
+        return 0
+
+    for step in prob_steps(far, far_bufs, 0, [0]):
+        step()
+    lax.fori_loop(0, last, far_loop, 0)
+    far_bwd(last, (near, near_bufs, 0))
     c_dkv = [copy(16 + d - 1, dkv.at[pl.ds(2 * d, 2)], rcv.at[d - 1], at_cp(rank + shards - d)) for d in range(1, shards)]
     for c in c_dkv:
         c.start()
-    lax.fori_loop(0, n_heads, near_bwd, 0)
+    lax.fori_loop(0, last, near_loop, 0)
+    near_bwd(last, None)
 
     for c in c_relay:
         c.wait_recv()
@@ -246,9 +365,9 @@
     c_o.wait_recv()
     rows = 128
     for i in range(cols // rows):
-        part = slice(i * rows, (i + 1) * rows)
-        y = dot_tn(o_s[0, :, :, part].reshape(hw, rows), flat(wo)) + dot_tn(og[:, :, part].reshape(hw, rows), flat(wop))
-        y_ref[part, :] = y.astype(BF16)
+        blk = slice(i * rows, (i + 1) * rows)
+        y = dot_tn(o_s[0, :, :, blk].reshape(hw, rows), flat(wo)) + dot_tn(og[:, :, blk].reshape(hw, rows), flat(wop))
+        y_ref[blk, :] = y.astype(BF16)
     for h in range(n_heads):
         go_ref[h] = (dot(o_s[0, h], dy_s[...]) + dot(o_s[1, h], dyp[...])).astype(BF16)
         gq_ref[h] = (dot(dq_s[0, h], x_s[...]) + dot(dq_s[1, h], xp[...])).astype(BF16)
@@ -268,11 +387,11 @@
     c_dq.wait_recv()
     c_last.wait_recv()
     for i in range(cols // rows):
-        part = slice(i * rows, (i + 1) * rows)
-        dx = dot_tn(dq_s[0, :, :, part].reshape(hw, rows), flat(wq)) + dot_tn(dqg[:, :, part].reshape(hw, rows), flat(wqp))
-        dx += dot_tn(dkvb[0, :hd, part], flat(wk)) + dot_tn(dkvb[0, hd:, part], flat(wv))
-        dx += dot_tn(dkvg[:hd, part], flat(wkp)) + dot_tn(dkvg[hd:, part], flat(wvp))
-        dx_ref[part, :] = dx.astype(BF16)
+        blk = slice(i * rows, (i + 1) * rows)
+        dx = dot_tn(dq_s[0, :, :, blk].reshape(hw, rows), flat(wq)) + dot_tn(dqg[:, :, blk].reshape(hw, rows), flat(wqp))
+        dx += dot_tn(dkvb[0, :hd, blk], flat(wk)) + dot_tn(dkvb[0, hd:, blk], flat(wv))
+        dx += dot_tn(dkvg[:hd, blk], flat(wkp)) + dot_tn(dkvg[hd:, blk], flat(wvp))
+        dx_ref[blk, :] = dx.astype(BF16)
     for c in [c_x, c_dy, c_o, c_dq, c_last] + c_w + c_relay + c_kv + c_dkv:
         c.wait_send()
 
@@ -303,7 +422,8 @@
             scratch_shapes=[b(cols, model)] * 4 + [b(2, hw // 2, model), b(2, hd // 2, model), b(2, hd // 2, model), b(2, hw // 2, model)] * 2
             + [b(*per_head), b(*per_head), b(*per_head), b(*per_head[1:]), b(*per_head), b(*per_head[1:]),
                b(2 * shards, 2 * hd, cols), b(2 * shards, cols, hd), b(2 * shards, cols, hd), f(*per_head),
-               f(2, n_heads, 1, cols), f(2, n_heads, 8, cols), f(6, cols, cols), f(2 * shards, 2 * hd, cols),
+               f(2, n_heads, 1, cols), f(2, n_heads, 8, cols), f(2, n_heads, 1, cols), f(2, 1, cols),
+               f(9, cols, cols), b(5, cols, cols), b(5, cols, cols), f(2 * shards, 2 * hd, cols),
                f(shards - 1, 2, 2 * hd, cols), b(2, 2 * hd, cols), b(2 * hd, cols),
                pltpu.SemaphoreType.DMA((N_COPIES,)), pltpu.SemaphoreType.DMA((N_COPIES,)), pltpu.SemaphoreType.DMA((6,))],
             compiler_params=pltpu.CompilerParams(vmem_limit_bytes=VMEM_LIMIT, collective_id=0, has_side_effects=True),

time: 133 us -> 132 us (level)
  no operation moved by 1% of the time
where the time goes in v1:
time: 132 us
  Pallas kernels  124 us (94%)
  local copies, waits for them, and re-layouts  7.19 us (5%)
    pallas_call x1, Pallas kernels, device_fn(): pl.pallas_call(functools.partial(kernel, shards, n_heads, hd, scale * mat...  124 us
    unnamed x16, local copies, waits for them, and re-layouts  7.19 us

profile of v1, /device:TPU:0, one launch (start us, length us, event | category | flops | bytes accessed | tf_op | source)
XLA Modules:
  0.0 131.7 jit_solution(9462889355506226129)
XLA Ops:
  0.6 123.8 %attention.1 = (bf16[512,896]{1,0:T(8,128)(2,1)}, bf16[512,896]{1,0:T(8,128)(2,1)}, bf16[7,64,896]{2,1,0:T(8,128)(2,1)}, bf16[64,896]{1,0:T(8,128)(2,1)}, bf16[6...) custom-call(bf16[512,896]{1,0:T(8,128)(2,1)} %x_hbm.1, bf16[512,896]{1,0:T(8,128)(2,1)} %dy_hbm.1, ...), custom_call_target="tpu_custom_call" | custom-call | flops 14797504512 | bytes 16777216 | tf_op jit(solution)/shard_map/attention/pallas_call | solution.py:415
  124.5 0.0 copy-start
  124.5 2.3 %copy.18 = bf16[512,896]{1,0:T(8,128)(2,1)} copy(bf16[512,896]{1,0:T(8,128)(2,1)} %get-tuple-element.24) | data formatting | bytes 1835008
  126.7 0.0 copy-done
  126.8 0.0 copy-start.2
  126.8 0.9 copy.19
  127.7 0.5 copy-done.2
  128.2 0.0 copy-start.4
  128.2 0.0 copy-start.1
  128.2 0.9 copy.20
  129.1 0.1 copy-done.4
  129.2 0.0 copy-start.3
  129.2 0.6 copy.21
  129.9 0.3 copy-done.3
  130.2 0.6 copy.22
  130.8 0.0 copy-done.1
  130.8 0.9 copy.23
Async XLA Ops:
  124.5 2.3 %copy-start = (bf16[512,896]{1,0:T(8,128)(2,1)S(1)}, bf16[512,896]{1,0:T(8,128)(2,1)}, u32[]{:S(2)}) copy-start(bf16[512,896]{1,0:T(8,128)(2,1)} %get-tuple-element.25) | copy-start | bytes 2752516
  126.8 1.5 %copy-start.2 = (bf16[7,64,896]{2,1,0:T(8,128)(2,1)S(1)}, bf16[7,64,896]{2,1,0:T(8,128)(2,1)}, u32[]{:S(2)}) copy-start(bf16[7,64,896]{2,1,0:T(8,128)(2,1)} %get-tuple-element.14) | copy-start | bytes 2408452
  128.2 1.0 copy-start.4
  128.2 2.6 %copy-start.1 = (bf16[7,64,896]{2,1,0:T(8,128)(2,1)S(1)}, bf16[7,64,896]{2,1,0:T(8,128)(2,1)}, u32[]{:S(2)}) copy-start(bf16[7,64,896]{2,1,0:T(8,128)(2,1)} %get-tuple-element.17) | copy-start | bytes 2408452
  129.2 0.9 copy-start.3

commit v2 on v1

--- a/solution.py
+++ b/solution.py
@@ -35,13 +35,10 @@
     return lax.dot_general(a, b, TN, preferred_element_type=F32)
 
 
-def far_units(rank, half, shards):
-    units = []
-    for d in range(1, shards):
-        early = (rank + shards - d) // shards
-        slot = early * half + (1 - early) * (1 - half)
-        units += [(slot, 2 * d + half, early), (1 - half, 2 * d + slot, 0)]
-    return units
+def shard_units(rank, half, d, shards):
+    early = (rank + shards - d) // shards
+    slot = early * half + (1 - early) * (1 - half)
+    return [(slot, 2 * d + half, early, False), (1 - half, 2 * d + slot, 0, False)]
 
 
 def diag_mask(size):
@@ -69,9 +66,9 @@
 def kernel(shards, n_heads, hd, c_scale, scale,
            x_hbm, dy_hbm, wq_hbm, wk_hbm, wv_hbm, wo_hbm,
            y_ref, dx_ref, gq_ref, gk_ref, gv_ref, go_ref,
-           x_s, xp, dy_s, dyp, wq, wk, wv, wo, wqp, wkp, wvp, wop,
+           x_s, xp, dy_s, dyp, w_own, w_peer,
            q_s, do_s, o_s, og, dq_s, dqg, kvt, k_s, v_s, acc, m_s, l_s, d_s, max_s, s_s, pb, db, dkv, rcv, dkvb, dkvg,
-           send, recv, local):
+           y_s, dx_s, dx_f, gq_s, gkv_s, go_s, send, recv, local):
     rank = lax.axis_index("cp")
     half = lax.axis_index("tp")
     core = rank % 2
@@ -80,6 +77,9 @@
     peer = {"tp": 1 - half}
     partner = {"cp": rank + 1 - 2 * core}
 
+    d_near = shards - 1 - 2 * core
+    d_far = (2, 1 + 2 * core)
+
     def at_cp(i):
         return {"cp": i % shards}
 
@@ -87,8 +87,19 @@
         return pltpu.make_async_remote_copy(src_ref=src, dst_ref=dst, send_sem=send.at[i], recv_sem=recv.at[i],
                                             device_id=device, device_id_type=pl.DeviceIdType.MESH)
 
-    loads = [pltpu.make_async_copy(src, dst, local.at[i]) for i, (src, dst) in enumerate(
-        [(x_hbm, x_s), (wk_hbm, wk), (wv_hbm, wv), (wq_hbm, wq), (wo_hbm, wo), (dy_hbm, dy_s)])]
+    n_o, n_k = hw // shards, hd // shards
+    w_rows = {"o": (0, n_o), "q": (n_o, n_o), "k": (2 * n_o, n_k), "v": (2 * n_o + n_k, n_k)}
+
+    def load(i, src, name):
+        start, size = w_rows[name]
+        return pltpu.make_async_copy(src, w_own.at[:, pl.ds(start, size), :], local.at[i])
+
+    def weight(ref, name):
+        start, size = w_rows[name]
+        return ref[:, start:start + size, :].reshape(shards * size, ref.shape[2])
+
+    loads = [pltpu.make_async_copy(x_hbm, x_s, local.at[0]), load(1, wk_hbm, "k"), load(2, wv_hbm, "v"), load(3, wq_hbm, "q"),
+             load(4, wo_hbm, "o"), pltpu.make_async_copy(dy_hbm, dy_s, local.at[5])]
     for c in loads:
         c.start()
     barrier = pltpu.get_barrier_semaphore()
@@ -97,21 +108,18 @@
         pl.semaphore_signal(barrier, inc=1, device_id=at_cp(rank + d), device_id_type=pl.DeviceIdType.MESH)
     pl.semaphore_wait(barrier, shards)
 
+    across = (rank + 2) % shards
     c_x = copy(0, x_hbm, xp, peer)
     c_dy = copy(1, dy_hbm, dyp, peer)
-    c_w = [copy(2 + i, src.at[core], dst.at[core], peer)
-           for i, (src, dst) in enumerate([(wo_hbm, wop), (wq_hbm, wqp), (wk_hbm, wkp), (wv_hbm, wvp)])]
-    c_relay = [copy(6 + i, dst.at[core], dst.at[core], partner) for i, dst in enumerate([wop, wqp, wkp, wvp])]
+    c_w = copy(2, w_own.at[rank], w_peer.at[rank], peer)
+    c_relay = [copy(3, w_peer.at[rank], w_peer.at[rank], partner), copy(4, w_peer.at[rank], w_peer.at[rank], at_cp(across)),
+               copy(5, w_peer.at[across], w_peer.at[across], partner)]
     c_x.start()
     c_dy.start()
-    for c in c_w:
-        c.start()
-
-    def flat(ref):
-        return ref[...].reshape(ref.shape[0] * ref.shape[1], ref.shape[2])
 
     def send_kv(slot):
-        cs = [copy(10 + 3 * slot + d - 1, kvt.at[slot], kvt.at[2 * d + slot], at_cp(rank + d)) for d in range(1, shards)]
+        ahead = (2, shards - 1 - 2 * core, 1 + 2 * core)
+        cs = [copy(10 + 3 * slot + i, kvt.at[slot], kvt.at[2 * d + slot], at_cp(rank + d)) for i, d in enumerate(ahead)]
         for c in cs:
             c.start()
         return cs
@@ -122,24 +130,26 @@
 
     for c in loads[:3]:
         c.wait()
-    kvt[0, :hd, :] = dot_nt(flat(wk), x_s[...]).astype(BF16)
-    kvt[0, hd:, :] = dot_nt(flat(wv), x_s[...]).astype(BF16)
+    kvt[0, :hd, :] = dot_nt(weight(w_own, "k"), x_s[...]).astype(BF16)
+    kvt[0, hd:, :] = dot_nt(weight(w_own, "v"), x_s[...]).astype(BF16)
     c_kv = send_kv(0)
     loads[3].wait()
-    q_s[0] = dot_nt(flat(wq), x_s[...]).astype(BF16).reshape(n_heads, hd, cols)
+    q_s[0] = dot_nt(weight(w_own, "q"), x_s[...]).astype(BF16).reshape(n_heads, hd, cols)
     loads[4].wait()
+    c_w.start()
     loads[5].wait()
-    do_s[0] = dot_nt(flat(wo), dy_s[...]).astype(BF16).reshape(n_heads, hd, cols)
+    do_s[0] = dot_nt(weight(w_own, "o"), dy_s[...]).astype(BF16).reshape(n_heads, hd, cols)
     keys_ready(0)
     c_x.wait_recv()
-    kvt[1, :hd, :] = dot_nt(flat(wk), xp[...]).astype(BF16)
-    kvt[1, hd:, :] = dot_nt(flat(wv), xp[...]).astype(BF16)
+    kvt[1, :hd, :] = dot_nt(weight(w_own, "k"), xp[...]).astype(BF16)
+    kvt[1, hd:, :] = dot_nt(weight(w_own, "v"), xp[...]).astype(BF16)
     c_kv += send_kv(1)
-    q_s[1] = dot_nt(flat(wq), xp[...]).astype(BF16).reshape(n_heads, hd, cols)
+    q_s[1] = dot_nt(weight(w_own, "q"), xp[...]).astype(BF16).reshape(n_heads, hd, cols)
     keys_ready(1)
 
-    near = [(half, half, 1, True), (1 - half, half, 0, False), (1 - half, 1 - half, 0, True)]
-    far = [u + (False,) for u in far_units(rank, half, shards)]
+    near = ([(half, half, 1, True), (1 - half, half, 0, False), (1 - half, 1 - half, 0, True)]
+            + shard_units(rank, half, d_near, shards))
+    far = shard_units(rank, half, d_far[0], shards) + shard_units(rank, half, d_far[1], shards)
     slots = (half, 1 - half)
     part = cols // 2
     triangle = diag_mask(part)
@@ -242,7 +252,7 @@
         copy(20, o_s.at[1, h], og.at[h], peer).start()
 
     def near_fwd(h, _):
-        forward(near, 6, h, True, (near, 6, h + 1))
+        forward(near, 4, h, True, (near, 4, h + 1))
         return 0
 
     def far_fwd(h, _):
@@ -252,22 +262,23 @@
 
     last = n_heads - 1
     maxes = {}
-    for step in score_steps(near, 6, 0, maxes):
+    for c in (c_kv[2], c_kv[5]):
+        c.wait_recv()
+    keys_ready(2 * d_near)
+    keys_ready(2 * d_near + 1)
+    for step in score_steps(near, 4, 0, maxes):
         step()
     score_max(near, maxes)
     lax.fori_loop(0, last, near_fwd, 0)
-    for i, c in enumerate(c_kv):
+    for c in (c_kv[0], c_kv[1], c_kv[3], c_kv[4]):
         c.wait_recv()
-    for tile in range(2, 2 * shards):
-        keys_ready(tile)
-    forward(near, 6, last, True, (far, 0, 0))
+    for d in d_far:
+        keys_ready(2 * d)
+        keys_ready(2 * d + 1)
+    forward(near, 4, last, True, (far, 0, 0))
     lax.fori_loop(0, last, far_fwd, 0)
-    for c in c_w:
-        c.wait_recv()
-    for c in c_relay:
-        c.start()
     c_dy.wait_recv()
-    do_s[1] = dot_nt(flat(wo), dyp[...]).astype(BF16).reshape(n_heads, hd, cols)
+    do_s[1] = dot_nt(weight(w_own, "o"), dyp[...]).astype(BF16).reshape(n_heads, hd, cols)
     forward(far, 0, last, False, None)
     send_o(last)
     dkv[...] = jnp.zeros_like(dkv)
@@ -353,47 +364,72 @@
         step()
     lax.fori_loop(0, last, far_loop, 0)
     far_bwd(last, (near, near_bufs, 0))
-    c_dkv = [copy(16 + d - 1, dkv.at[pl.ds(2 * d, 2)], rcv.at[d - 1], at_cp(rank + shards - d)) for d in range(1, shards)]
-    for c in c_dkv:
+    c_dkv = [copy(16 + i, dkv.at[pl.ds(2 * d, 2)], rcv.at[i], at_cp(rank + shards - d)) for i, d in enumerate(d_far + (d_near,))]
+    for c in c_dkv[:2]:
+        c.start()
+    c_w.wait_recv()
+    for c in c_relay[:2]:
         c.start()
     lax.fori_loop(0, last, near_loop, 0)
     near_bwd(last, None)
-
-    for c in c_relay:
-        c.wait_recv()
-    c_o = copy(20, o_s.at[1], og, peer)
-    c_o.wait_recv()
-    rows = 128
-    for i in range(cols // rows):
-        blk = slice(i * rows, (i + 1) * rows)
-        y = dot_tn(o_s[0, :, :, blk].reshape(hw, rows), flat(wo)) + dot_tn(og[:, :, blk].reshape(hw, rows), flat(wop))
-        y_ref[blk, :] = y.astype(BF16)
+    c_dkv[2].start()
+    c_relay[1].wait_recv()
+    c_relay[2].start()
+
+    stores = []
+
+    def leave(src, dst):
+        c = pltpu.make_async_copy(src, dst, local.at[6 + len(stores)])
+        c.start()
+        stores.append(c)
+
     for h in range(n_heads):
-        go_ref[h] = (dot(o_s[0, h], dy_s[...]) + dot(o_s[1, h], dyp[...])).astype(BF16)
-        gq_ref[h] = (dot(dq_s[0, h], x_s[...]) + dot(dq_s[1, h], xp[...])).astype(BF16)
-
+        go_s[h] = (dot(o_s[0, h], dy_s[...]) + dot(o_s[1, h], dyp[...])).astype(BF16)
+    leave(go_s, go_ref)
     for c in c_dkv:
         c.wait_recv()
     for slot in (1, 0):
         total = dkv[slot] + rcv[0, slot] + rcv[1, slot] + rcv[2, slot]
         dkvb[slot, :hd, :] = (total[:hd, :] * scale).astype(BF16)
         dkvb[slot, hd:, :] = total[hd:, :].astype(BF16)
-    c_last = copy(19, dkvb.at[1], dkvg, peer)
-    c_last.start()
-    gkv = dot(dkvb[0], x_s[...]) + dot(dkvb[1], xp[...])
-    gk_ref[...] = gkv[:hd, :].astype(BF16)
-    gv_ref[...] = gkv[hd:, :].astype(BF16)
+        if slot == 1:
+            c_last = copy(19, dkvb.at[1], dkvg, peer)
+            c_last.start()
+    for h in range(n_heads):
+        gq_s[h] = (dot(dq_s[0, h], x_s[...]) + dot(dq_s[1, h], xp[...])).astype(BF16)
+    leave(gq_s, gq_ref)
+    gkv_s[...] = (dot(dkvb[0], x_s[...]) + dot(dkvb[1], xp[...])).astype(BF16)
+    leave(gkv_s.at[:hd], gk_ref)
+    leave(gkv_s.at[hd:], gv_ref)
+    c_o = copy(20, o_s.at[1], og, peer)
+    c_o.wait_recv()
+    c_relay[0].wait_recv()
+    c_relay[2].wait_recv()
+    rows = 128
+    for i in range(cols // rows):
+        blk = slice(i * rows, (i + 1) * rows)
+        y = (dot_tn(o_s[0, :, :, blk].reshape(hw, rows), weight(w_own, "o"))
+             + dot_tn(og[:, :, blk].reshape(hw, rows), weight(w_peer, "o")))
+        y_s[blk, :] = y.astype(BF16)
+    leave(y_s, y_ref)
     c_dq = copy(21, dq_s.at[1], dqg, peer)
     c_dq.wait_recv()
+    for i in range(cols // rows):
+        blk = slice(i * rows, (i + 1) * rows)
+        dx = (dot_tn(dq_s[0, :, :, blk].reshape(hw, rows), weight(w_own, "q"))
+              + dot_tn(dqg[:, :, blk].reshape(hw, rows), weight(w_peer, "q")))
+        dx += dot_tn(dkvb[0, :hd, blk], weight(w_own, "k")) + dot_tn(dkvb[0, hd:, blk], weight(w_own, "v"))
+        dx_f[blk, :] = dx
     c_last.wait_recv()
     for i in range(cols // rows):
         blk = slice(i * rows, (i + 1) * rows)
-        dx = dot_tn(dq_s[0, :, :, blk].reshape(hw, rows), flat(wq)) + dot_tn(dqg[:, :, blk].reshape(hw, rows), flat(wqp))
-        dx += dot_tn(dkvb[0, :hd, blk], flat(wk)) + dot_tn(dkvb[0, hd:, blk], flat(wv))
-        dx += dot_tn(dkvg[:hd, blk], flat(wkp)) + dot_tn(dkvg[hd:, blk], flat(wvp))
-        dx_ref[blk, :] = dx.astype(BF16)
-    for c in [c_x, c_dy, c_o, c_dq, c_last] + c_w + c_relay + c_kv + c_dkv:
+        dx = dx_f[blk, :] + dot_tn(dkvg[:hd, blk], weight(w_peer, "k")) + dot_tn(dkvg[hd:, blk], weight(w_peer, "v"))
+        dx_s[blk, :] = dx.astype(BF16)
+    leave(dx_s, dx_ref)
+    for c in [c_x, c_dy, c_o, c_dq, c_last, c_w] + c_relay + c_kv + c_dkv:
         c.wait_send()
+    for c in stores:
+        c.wait()
 
 
 def solution(mesh):
@@ -404,10 +440,10 @@
         cols = x_own.shape[0]
         hw = n_heads * hd
         scale = hd ** -0.5
-        wq = w_query.transpose(1, 2, 0).reshape(2, hw // 2, model)
-        wk = w_key.transpose(1, 2, 0).reshape(2, hd // 2, model)
-        wv = w_value.transpose(1, 2, 0).reshape(2, hd // 2, model)
-        wo = w_out.reshape(2, hw // 2, model)
+        wq = w_query.transpose(1, 2, 0).reshape(shards, hw // shards, model)
+        wk = w_key.transpose(1, 2, 0).reshape(shards, hd // shards, model)
+        wv = w_value.transpose(1, 2, 0).reshape(shards, hd // shards, model)
+        wo = w_out.reshape(shards, hw // shards, model)
         per_head = (2, n_heads, hd, cols)
         b = lambda *s: pltpu.VMEM(s, BF16)
         f = lambda *s: pltpu.VMEM(s, F32)
@@ -418,14 +454,15 @@
                        jax.ShapeDtypeStruct((n_heads, hd, model), BF16), jax.ShapeDtypeStruct((hd, model), BF16),
                        jax.ShapeDtypeStruct((hd, model), BF16), jax.ShapeDtypeStruct((n_heads, hd, model), BF16)),
             in_specs=[ANY] * 6,
-            out_specs=(VMEM,) * 6,
-            scratch_shapes=[b(cols, model)] * 4 + [b(2, hw // 2, model), b(2, hd // 2, model), b(2, hd // 2, model), b(2, hw // 2, model)] * 2
+            out_specs=(ANY,) * 6,
+            scratch_shapes=[b(cols, model)] * 4 + [b(shards, 2 * (hw + hd) // shards, model)] * 2
             + [b(*per_head), b(*per_head), b(*per_head), b(*per_head[1:]), b(*per_head), b(*per_head[1:]),
                b(2 * shards, 2 * hd, cols), b(2 * shards, cols, hd), b(2 * shards, cols, hd), f(*per_head),
                f(2, n_heads, 1, cols), f(2, n_heads, 8, cols), f(2, n_heads, 1, cols), f(2, 1, cols),
                f(9, cols, cols), b(5, cols, cols), b(5, cols, cols), f(2 * shards, 2 * hd, cols),
                f(shards - 1, 2, 2 * hd, cols), b(2, 2 * hd, cols), b(2 * hd, cols),
-               pltpu.SemaphoreType.DMA((N_COPIES,)), pltpu.SemaphoreType.DMA((N_COPIES,)), pltpu.SemaphoreType.DMA((6,))],
+               b(cols, model), b(cols, model), f(cols, model), b(n_heads, hd, model), b(2 * hd, model), b(n_heads, hd, model),
+               pltpu.SemaphoreType.DMA((N_COPIES,)), pltpu.SemaphoreType.DMA((N_COPIES,)), pltpu.SemaphoreType.DMA((12,))],
             compiler_params=pltpu.CompilerParams(vmem_limit_bytes=VMEM_LIMIT, collective_id=0, has_side_effects=True),
             cost_estimate=pl.CostEstimate(flops=area * 7 * 2 * hd, bytes_accessed=16 << 20, transcendentals=2 * area),
             name="attention",

time: 132 us -> 116 us (0.88)
  Pallas kernels: 124 us -> 108 us
    pallas_call x1, Pallas kernels: 124 us -> 108 us  [device_fn(): pl.pallas_call(functools.partial(kernel, shards, n_heads, hd, scale * mat...]
where the time goes in v2:
time: 116 us
  Pallas kernels  108 us (93%)
  local copies, waits for them, and re-layouts  7.19 us (6%)
    pallas_call x1, Pallas kernels, device_fn(): pl.pallas_call(functools.partial(kernel, shards, n_heads, hd, scale * mat...  108 us
    unnamed x16, local copies, waits for them, and re-layouts  7.19 us

profile of v2, /device:TPU:0, one launch (start us, length us, event | category | flops | bytes accessed | tf_op | source)
XLA Modules:
  0.0 115.5 jit_solution(12565297369607130745)
XLA Ops:
  0.6 107.7 %attention.1 = (bf16[512,896]{1,0:T(8,128)(2,1)}, bf16[512,896]{1,0:T(8,128)(2,1)}, bf16[7,64,896]{2,1,0:T(8,128)(2,1)}, bf16[64,896]{1,0:T(8,128)(2,1)}, bf16[6...) custom-call(bf16[512,896]{1,0:T(8,128)(2,1)} %x_hbm.1, bf16[512,896]{1,0:T(8,128)(2,1)} %dy_hbm.1, ...), custom_call_target="tpu_custom_call" | custom-call | flops 14797504512 | bytes 16777216 | tf_op jit(solution)/shard_map/attention/pallas_call | solution.py:451
  108.3 0.0 copy-start
  108.4 2.3 %copy.18 = bf16[512,896]{1,0:T(8,128)(2,1)} copy(bf16[512,896]{1,0:T(8,128)(2,1)} %get-tuple-element.24) | data formatting | bytes 1835008
  110.6 0.0 copy-done
  110.6 0.0 copy-start.2
  110.6 0.9 copy.19
  111.5 0.5 copy-done.2
  112.1 0.0 copy-start.4
  112.1 0.0 copy-start.1
  112.1 0.9 copy.20
  113.0 0.1 copy-done.4
  113.1 0.0 copy-start.3
  113.1 0.6 copy.21
  113.7 0.3 copy-done.3
  114.0 0.6 copy.22
  114.7 0.0 copy-done.1
  114.7 0.9 copy.23
Async XLA Ops:
  108.3 2.3 %copy-start = (bf16[512,896]{1,0:T(8,128)(2,1)S(1)}, bf16[512,896]{1,0:T(8,128)(2,1)}, u32[]{:S(2)}) copy-start(bf16[512,896]{1,0:T(8,128)(2,1)} %get-tuple-element.25) | copy-start | bytes 2752516
  110.6 1.5 %copy-start.2 = (bf16[7,64,896]{2,1,0:T(8,128)(2,1)S(1)}, bf16[7,64,896]{2,1,0:T(8,128)(2,1)}, u32[]{:S(2)}) copy-start(bf16[7,64,896]{2,1,0:T(8,128)(2,1)} %get-tuple-element.14) | copy-start | bytes 2408452
  112.1 1.0 copy-start.4
  112.1 2.6 %copy-start.1 = (bf16[7,64,896]{2,1,0:T(8,128)(2,1)S(1)}, bf16[7,64,896]{2,1,0:T(8,128)(2,1)}, u32[]{:S(2)}) copy-start(bf16[7,64,896]{2,1,0:T(8,128)(2,1)} %get-tuple-element.17) | copy-start | bytes 2408452
  113.1 0.9 copy-start.3

commit v3 on v2

--- a/solution.py
+++ b/solution.py
@@ -19,8 +19,8 @@
 TN = (((0,), (0,)), ((), ()))
 VMEM = pl.BlockSpec(memory_space=pltpu.VMEM)
 ANY = pl.BlockSpec(memory_space=pl.ANY)
-VMEM_LIMIT = 64 * 1024 * 1024
-N_COPIES = 22
+VMEM_LIMIT = 52 * 1024 * 1024
+N_COPIES = 23
 
 
 def dot(a, b):
@@ -109,13 +109,14 @@
     pl.semaphore_wait(barrier, shards)
 
     across = (rank + 2) % shards
-    c_x = copy(0, x_hbm, xp, peer)
+    mid = cols // 2
+    c_x = [copy(i, x_hbm.at[pl.ds(j * mid, mid)], xp.at[pl.ds(j * mid, mid)], peer) for i, j in ((0, 0), (22, 1))]
     c_dy = copy(1, dy_hbm, dyp, peer)
     c_w = copy(2, w_own.at[rank], w_peer.at[rank], peer)
     c_relay = [copy(3, w_peer.at[rank], w_peer.at[rank], partner), copy(4, w_peer.at[rank], w_peer.at[rank], at_cp(across)),
                copy(5, w_peer.at[across], w_peer.at[across], partner)]
-    c_x.start()
-    c_dy.start()
+    for c in c_x + [c_dy]:
+        c.start()
 
     def send_kv(slot):
         ahead = (2, shards - 1 - 2 * core, 1 + 2 * core)
@@ -140,11 +141,14 @@
     loads[5].wait()
     do_s[0] = dot_nt(weight(w_own, "o"), dy_s[...]).astype(BF16).reshape(n_heads, hd, cols)
     keys_ready(0)
-    c_x.wait_recv()
-    kvt[1, :hd, :] = dot_nt(weight(w_own, "k"), xp[...]).astype(BF16)
-    kvt[1, hd:, :] = dot_nt(weight(w_own, "v"), xp[...]).astype(BF16)
-    c_kv += send_kv(1)
-    q_s[1] = dot_nt(weight(w_own, "q"), xp[...]).astype(BF16).reshape(n_heads, hd, cols)
+    for j, c in enumerate(c_x):
+        q = slice(j * mid, (j + 1) * mid)
+        c.wait_recv()
+        kvt[1, :hd, q] = dot_nt(weight(w_own, "k"), xp[q, :]).astype(BF16)
+        kvt[1, hd:, q] = dot_nt(weight(w_own, "v"), xp[q, :]).astype(BF16)
+        if j == 1:
+            c_kv += send_kv(1)
+        q_s[1, :, :, q] = dot_nt(weight(w_own, "q"), xp[q, :]).astype(BF16).reshape(n_heads, hd, mid)
     keys_ready(1)
 
     near = ([(half, half, 1, True), (1 - half, half, 0, False), (1 - half, 1 - half, 0, True)]
@@ -352,29 +356,49 @@
             dq_s[slots[g], h] = ((dq[g] + acc[slots[g], h]) * scale).astype(BF16)
         copy(21, dq_s.at[1, h], dqg.at[h], peer).start()
 
+    c_pair = copy(16, dkv.at[pl.ds(2 * d_far[1], 2)], rcv.at[0], partner)
+    c_cross = copy(17, dkv.at[pl.ds(2 * d_far[0], 2)], rcv.at[1], at_cp(across))
+    c_near = copy(18, dkv.at[pl.ds(2 * d_near, 2)], rcv.at[2], partner)
+
     def far_loop(h, _):
         far_bwd(h, (far, far_bufs, h + 1))
+
+        @pl.when(h == 3)
+        def _():
+            c_w.wait_recv()
+            c_relay[0].start()
+            c_relay[1].start()
+
         return 0
 
     def near_loop(h, _):
         near_bwd(h, (near, near_bufs, h + 1))
+
+        @pl.when(h == 0)
+        def _():
+            c_pair.wait_recv()
+            for slot in (0, 1):
+                dkv[2 * d_far[0] + slot] += rcv[0, slot]
+
+        @pl.when(h == 1)
+        def _():
+            c_cross.start()
+
+        @pl.when(h == 3)
+        def _():
+            c_relay[1].wait_recv()
+            c_relay[2].start()
+
         return 0
 
     for step in prob_steps(far, far_bufs, 0, [0]):
         step()
     lax.fori_loop(0, last, far_loop, 0)
     far_bwd(last, (near, near_bufs, 0))
-    c_dkv = [copy(16 + i, dkv.at[pl.ds(2 * d, 2)], rcv.at[i], at_cp(rank + shards - d)) for i, d in enumerate(d_far + (d_near,))]
-    for c in c_dkv[:2]:
-        c.start()
-    c_w.wait_recv()
-    for c in c_relay[:2]:
-        c.start()
+    c_pair.start()
     lax.fori_loop(0, last, near_loop, 0)
     near_bwd(last, None)
-    c_dkv[2].start()
-    c_relay[1].wait_recv()
-    c_relay[2].start()
+    c_near.start()
 
     stores = []
 
@@ -383,20 +407,24 @@
         c.start()
         stores.append(c)
 
-    for h in range(n_heads):
-        go_s[h] = (dot(o_s[0, h], dy_s[...]) + dot(o_s[1, h], dyp[...])).astype(BF16)
+    def weight_grad(out, grads, own, other):
+        for start in range(0, own.shape[1], 256):
+            c = slice(start, min(start + 256, own.shape[1]))
+            g = dot(grads[0].reshape(hw, cols), own[:, c]) + dot(grads[1].reshape(hw, cols), other[:, c])
+            out[:, :, c] = g.astype(BF16).reshape(n_heads, hd, g.shape[1])
+
+    weight_grad(go_s, o_s, dy_s, dyp)
     leave(go_s, go_ref)
-    for c in c_dkv:
-        c.wait_recv()
+    c_cross.wait_recv()
+    c_near.wait_recv()
     for slot in (1, 0):
-        total = dkv[slot] + rcv[0, slot] + rcv[1, slot] + rcv[2, slot]
+        total = dkv[slot] + rcv[1, slot] + rcv[2, slot]
         dkvb[slot, :hd, :] = (total[:hd, :] * scale).astype(BF16)
         dkvb[slot, hd:, :] = total[hd:, :].astype(BF16)
         if slot == 1:
             c_last = copy(19, dkvb.at[1], dkvg, peer)
             c_last.start()
-    for h in range(n_heads):
-        gq_s[h] = (dot(dq_s[0, h], x_s[...]) + dot(dq_s[1, h], xp[...])).astype(BF16)
+    weight_grad(gq_s, dq_s, x_s, xp)
     leave(gq_s, gq_ref)
     gkv_s[...] = (dot(dkvb[0], x_s[...]) + dot(dkvb[1], xp[...])).astype(BF16)
     leave(gkv_s.at[:hd], gk_ref)
@@ -426,7 +454,7 @@
         dx = dx_f[blk, :] + dot_tn(dkvg[:hd, blk], weight(w_peer, "k")) + dot_tn(dkvg[hd:, blk], weight(w_peer, "v"))
         dx_s[blk, :] = dx.astype(BF16)
     leave(dx_s, dx_ref)
-    for c in [c_x, c_dy, c_o, c_dq, c_last, c_w] + c_relay + c_kv + c_dkv:
+    for c in c_x + [c_dy, c_o, c_dq, c_last, c_w, c_pair, c_cross, c_near] + c_relay + c_kv:
         c.wait_send()
     for c in stores:
         c.wait()

time: 116 us -> 101 us (0.87)
  Pallas kernels: 108 us -> 92.1 us
    pallas_call x1, Pallas kernels: 108 us -> 92.1 us  [device_fn(): pl.pallas_call(functools.partial(kernel, shards, n_heads, hd, scale * mat...]
    unnamed x16 -> x14, local copies, waits for them, and re-layouts: 7.19 us -> 8.03 us
where the time goes in v3:
time: 101 us
  Pallas kernels  92.1 us (91%)
  local copies, waits for them, and re-layouts  8.03 us (8%)
    pallas_call x1, Pallas kernels, device_fn(): pl.pallas_call(functools.partial(kernel, shards, n_heads, hd, scale * mat...  92.1 us
    unnamed x14, local copies, waits for them, and re-layouts  8.03 us

profile of v3, /device:TPU:0, one launch (start us, length us, event | category | flops | bytes accessed | tf_op | source)
XLA Modules:
  0.0 100.8 jit_solution(4161790355517824925)
XLA Ops:
  0.6 0.0 copy-start
  0.6 0.9 copy-done
  1.5 0.0 copy-start.1
  1.5 0.9 copy-done.1
  2.4 92.1 %attention.1 = (bf16[512,896]{1,0:T(8,128)(2,1)}, bf16[512,896]{1,0:T(8,128)(2,1)}, bf16[7,64,896]{2,1,0:T(8,128)(2,1)S(1)}, bf16[64,896]{1,0:T(8,128)(2,1)S(1)}...) custom-call(bf16[512,896]{1,0:T(8,128)(2,1)} %x_hbm.1, bf16[512,896]{1,0:T(8,128)(2,1)} %dy_hbm.1, ...), custom_call_target="tpu_custom_call" | custom-call | flops 14797504512 | bytes 16777216 | tf_op jit(solution)/shard_map/attention/pallas_call | solution.py:479
  94.6 0.0 copy-start.2
  94.6 2.3 %copy.18 = bf16[512,896]{1,0:T(8,128)(2,1)} copy(bf16[512,896]{1,0:T(8,128)(2,1)} %get-tuple-element.24) | data formatting | bytes 1835008
  96.8 0.0 copy-done.2
  96.8 0.9 copy.19
  97.8 0.0 copy-start.3
  97.8 0.9 copy.20
  98.6 0.6 copy.21
  99.3 0.6 copy.22
  99.9 0.0 copy-done.3
  99.9 0.9 copy.23
Async XLA Ops:
  0.6 0.9 copy-start
  1.5 0.9 copy-start.1
  94.6 2.3 %copy-start.2 = (bf16[512,896]{1,0:T(8,128)(2,1)S(1)}, bf16[512,896]{1,0:T(8,128)(2,1)}, u32[]{:S(2)}) copy-start(bf16[512,896]{1,0:T(8,128)(2,1)} %get-tuple-element.25) | copy-start | bytes 2752516
  97.8 2.2 %copy-start.3 = (bf16[7,64,896]{2,1,0:T(8,128)(2,1)S(1)}, bf16[7,64,896]{2,1,0:T(8,128)(2,1)}, u32[]{:S(2)}) copy-start(bf16[7,64,896]{2,1,0:T(8,128)(2,1)} %get-tuple-element.17) | copy-start | bytes 2408452

commit v4 on v3

--- a/solution.py
+++ b/solution.py
@@ -19,8 +19,11 @@
 TN = (((0,), (0,)), ((), ()))
 VMEM = pl.BlockSpec(memory_space=pltpu.VMEM)
 ANY = pl.BlockSpec(memory_space=pl.ANY)
-VMEM_LIMIT = 52 * 1024 * 1024
+HBM = pl.BlockSpec(memory_space=pltpu.HBM)
+VMEM_LIMIT = 64 * 1024 * 1024 - 64 * 1024
 N_COPIES = 23
+PAD = 16
+BIG = 3.0e38
 
 
 def dot(a, b):
@@ -63,11 +66,20 @@
     return x.astype(F32).T.astype(BF16)
 
 
+def with_columns(x_t, row):
+    hi = jnp.clip(row, -BIG, BIG).astype(BF16).astype(F32)
+    mid = (row - hi).astype(BF16).astype(F32)
+    low = row - hi - mid
+    line = lax.broadcasted_iota(jnp.int32, (PAD, row.shape[1]), 0)
+    extra = jnp.where(line == 0, hi, jnp.where(line == 1, mid, jnp.where(line == 2, low, 0.0)))
+    return jnp.concatenate([x_t.astype(F32), extra], axis=0).T.astype(BF16)
+
+
 def kernel(shards, n_heads, hd, c_scale, scale,
            x_hbm, dy_hbm, wq_hbm, wk_hbm, wv_hbm, wo_hbm,
            y_ref, dx_ref, gq_ref, gk_ref, gv_ref, go_ref,
            x_s, xp, dy_s, dyp, w_own, w_peer,
-           q_s, do_s, o_s, og, dq_s, dqg, kvt, k_s, v_s, acc, m_s, l_s, d_s, max_s, s_s, pb, db, dkv, rcv, dkvb, dkvg,
+           q_s, do_s, o_s, og, dq_s, dqg, kvt, k_s, ka, q_n, do_n, acc, m_s, l_s, max_s, s_s, pb, db, dkv, rcv, dkvb, dkvg,
            y_s, dx_s, dx_f, gq_s, gkv_s, go_s, send, recv, local):
     rank = lax.axis_index("cp")
     half = lax.axis_index("tp")
@@ -127,7 +139,10 @@
 
     def keys_ready(tile):
         k_s[tile] = transpose_bf16(kvt[tile, :hd, :])
-        v_s[tile] = transpose_bf16(kvt[tile, hd:, :])
+        minus = jnp.where(lax.broadcasted_iota(jnp.int32, (PAD, cols), 0) < 3, -1.0, 0.0).astype(BF16)
+        for i in (0, 1):
+            ka[tile, i, :hd, :] = kvt[tile, i * hd:(i + 1) * hd, :]
+            ka[tile, i, hd:, :] = minus
 
     for c in loads[:3]:
         c.wait()
@@ -239,7 +254,7 @@
                 else:
                     l_row = jnp.sum(l[g], axis=0, keepdims=True)
                     o_s[slots[g], h] = (o[g] / l_row).astype(BF16)
-                    m_s[slots[g], h] = m[g] + jnp.log2(l_row)
+                    q_n[slots[g], h] = with_columns(q_s[slots[g], h], (m[g] + jnp.log2(l_row)) * (1.0 / c_scale))
 
         return [functools.partial(step, u, c) for u in range(len(units)) for c in (0, 1)], finish
 
@@ -287,23 +302,30 @@
     send_o(last)
     dkv[...] = jnp.zeros_like(dkv)
 
-    def row_dots(h, _):
-        for s in (0, 1):
-            d_s[s, h] = jnp.sum(do_s[s, h].astype(F32) * o_s[s, h].astype(F32), axis=0, keepdims=True)
-        return 0
-
-    lax.fori_loop(0, n_heads, row_dots, 0)
-
-    def prob_steps(units, bufs, h, which):
-        def step(u, c):
-            qi, kt, first, diag = units[u]
-            r, q = spans(diag, c)
-            buf = bufs[u % len(bufs)]
-            p = jnp.exp2(dot(k_s[kt, r], q_s[qi, h, :, q]) * c_scale - m_s[qi, h, :, q])
-            p = masked(p, diag, 0.0)
-            pb[buf, r, q] = p.astype(BF16)
-            db[buf, r, q] = (p * (dot(v_s[kt, r], do_s[qi, h, :, q]) - d_s[qi, h, :, q])).astype(BF16)
-        return [functools.partial(step, u, c) for u in which for c in (0, 1)]
+    for h in range(n_heads):
+        for i in (0, 1):
+            delta = jnp.sum(do_s[i, h].astype(F32) * o_s[i, h].astype(F32), axis=0, keepdims=True)
+            do_n[i, h] = with_columns(do_s[i, h], delta)
+    lower = lax.broadcasted_iota(jnp.int32, (part, part), 0) >= lax.broadcasted_iota(jnp.int32, (part, part), 1)
+
+    def prob_steps(units, bufs, h, u):
+        qi, kt, first, diag = units[u]
+        buf = bufs[u % len(bufs)]
+        kept = {}
+
+        def probs(c):
+            r, k = slice(c * part, (c + 1) * part), slice(0, part if diag and c == 0 else cols)
+            p = jnp.exp2(dot(q_n[qi, h, r], ka[kt, 0, :, k]) * c_scale)
+            if diag:
+                p = jnp.concatenate([p[:, :c * part], jnp.where(lower, p[:, c * part:], 0.0)], axis=1) if c else jnp.where(lower, p, 0.0)
+            pb[buf, r, k] = p.astype(BF16)
+            kept[c] = p
+
+        def grads(c):
+            r, k = slice(c * part, (c + 1) * part), slice(0, part if diag and c == 0 else cols)
+            db[buf, r, k] = (kept[c] * dot(do_n[qi, h, r], ka[kt, 1, :, k])).astype(BF16)
+
+        return [functools.partial(f, c) for c in (0, 1) for f in (probs, grads)]
 
     def grad_steps(units, bufs, h, u, dq):
         qi, kt, first, diag = units[u]
@@ -311,19 +333,18 @@
         kept = {}
 
         def over_queries(name, src, lhs, rows, c):
-            q = slice(c * part, (c + 1) * part)
-            keys = slice(0, part) if diag and c == 0 else slice(0, cols)
-            val = dot_nt(lhs[qi, h, :, q], src[buf, keys, q])
-            if c == 0 and not diag:
+            q, k = slice(c * part, (c + 1) * part), slice(0, part if diag and c == 0 else cols)
+            val = dot(lhs[qi, h, :, q], src[buf, q, k])
+            if diag:
+                dkv[kt, rows, k] += val
+            elif c == 0:
                 kept[name] = val
-            elif diag:
-                dkv[kt, rows, keys] += val
             else:
                 dkv[kt, rows, :] += kept[name] + val
 
         def over_keys(c):
-            r, q = spans(diag, c)
-            val = widen(dot(kvt[kt, :hd, r], db[buf, r, q]), 0.0)
+            k, q = spans(diag, c)
+            val = widen(dot_nt(kvt[kt, :hd, k], db[buf, q, k]), 0.0)
             if c == 0:
                 kept["q"] = val
             else:
@@ -337,10 +358,14 @@
         dq = [jnp.zeros((hd, cols), F32), jnp.zeros((hd, cols), F32)]
         for u in range(len(units)):
             if u + 1 < len(units):
-                ahead = prob_steps(units, bufs, h, [u + 1])
+                ahead = prob_steps(units, bufs, h, u + 1)
             else:
-                ahead = prob_steps(*nxt, [0]) if nxt else []
-            interleave(ahead, grad_steps(units, bufs, h, u, dq))
+                ahead = prob_steps(*nxt, 0) if nxt else []
+            products = grad_steps(units, bufs, h, u, dq)
+            for i, step in enumerate(products):
+                step()
+                if i < len(ahead):
+                    ahead[i]()
         return dq
 
     near_bufs, far_bufs = (0, 1, 2), (3, 4)
@@ -391,7 +416,7 @@
 
         return 0
 
-    for step in prob_steps(far, far_bufs, 0, [0]):
+    for step in prob_steps(far, far_bufs, 0, 0):
         step()
     lax.fori_loop(0, last, far_loop, 0)
     far_bwd(last, (near, near_bufs, 0))
@@ -460,6 +485,19 @@
         c.wait()
 
 
+def hand_out(n, *refs):
+    src, dst, held, sems = refs[:n], refs[n:2 * n], refs[2 * n:3 * n], refs[3 * n]
+    loads = [pltpu.make_async_copy(src[i], held[i], sems.at[0, i]) for i in range(n)]
+    stores = [pltpu.make_async_copy(held[i], dst[i], sems.at[1, i]) for i in range(n)]
+    for c in loads:
+        c.start()
+    for load, store in zip(loads, stores):
+        load.wait()
+        store.start()
+    for c in stores:
+        c.wait()
+
+
 def solution(mesh):
     shards = mesh.shape["cp"]
 
@@ -481,12 +519,13 @@
             out_shape=(jax.ShapeDtypeStruct((cols, model), BF16), jax.ShapeDtypeStruct((cols, model), BF16),
                        jax.ShapeDtypeStruct((n_heads, hd, model), BF16), jax.ShapeDtypeStruct((hd, model), BF16),
                        jax.ShapeDtypeStruct((hd, model), BF16), jax.ShapeDtypeStruct((n_heads, hd, model), BF16)),
-            in_specs=[ANY] * 6,
+            in_specs=[HBM] * 6,
             out_specs=(ANY,) * 6,
             scratch_shapes=[b(cols, model)] * 4 + [b(shards, 2 * (hw + hd) // shards, model)] * 2
             + [b(*per_head), b(*per_head), b(*per_head), b(*per_head[1:]), b(*per_head), b(*per_head[1:]),
-               b(2 * shards, 2 * hd, cols), b(2 * shards, cols, hd), b(2 * shards, cols, hd), f(*per_head),
-               f(2, n_heads, 1, cols), f(2, n_heads, 8, cols), f(2, n_heads, 1, cols), f(2, 1, cols),
+               b(2 * shards, 2 * hd, cols), b(2 * shards, cols, hd), b(2 * shards, 2, hd + PAD, cols),
+               b(2, n_heads, cols, hd + PAD), b(2, n_heads, cols, hd + PAD), f(*per_head),
+               f(2, n_heads, 1, cols), f(2, n_heads, 8, cols), f(2, 1, cols),
                f(9, cols, cols), b(5, cols, cols), b(5, cols, cols), f(2 * shards, 2 * hd, cols),
                f(shards - 1, 2, 2 * hd, cols), b(2, 2 * hd, cols), b(2 * hd, cols),
                b(cols, model), b(cols, model), f(cols, model), b(n_heads, hd, model), b(2 * hd, model), b(n_heads, hd, model),
@@ -495,6 +534,16 @@
             cost_estimate=pl.CostEstimate(flops=area * 7 * 2 * hd, bytes_accessed=16 << 20, transcendentals=2 * area),
             name="attention",
         )(x_own, dy_own, wq, wk, wv, wo)
+        outs = (y, dx, gq, gk, gv, go)
+        y, dx, gq, gk, gv, go = pl.pallas_call(
+            functools.partial(hand_out, len(outs)),
+            out_shape=tuple(jax.ShapeDtypeStruct(o.shape, o.dtype) for o in outs),
+            in_specs=[HBM] * len(outs),
+            out_specs=(HBM,) * len(outs),
+            scratch_shapes=[pltpu.VMEM(o.shape, o.dtype) for o in outs] + [pltpu.SemaphoreType.DMA((2, len(outs)))],
+            cost_estimate=pl.CostEstimate(flops=0, bytes_accessed=8 << 20, transcendentals=0),
+            name="hand_out",
+        )(*outs)
         back = lambda g, n: g.reshape(n, hd, model).transpose(2, 0, 1)[None]
         return y, dx, back(gq, n_heads), back(gk, 1), back(gv, 1), go[None]
 

time: 101 us -> 93.3 us (0.924)
  local copies, waits for them, and re-layouts: 8.03 us -> 0 us
    unnamed x14 -> x0, local copies, waits for them, and re-layouts: 8.03 us -> none
    pallas_call x0 -> x1, Pallas kernels: none -> 3.11 us  [device_fn(): pl.pallas_call(functools.partial(hand_out, len(outs)), out_shape=tuple((j...]
    pallas_call x1, Pallas kernels: 92.1 us -> 89.3 us  [device_fn(): pl.pallas_call(functools.partial(kernel, shards, n_heads, hd, scale * mat...]
where the time goes in v4:
time: 93.3 us; the launch traced here: 93.2 us
  Pallas kernels  92.4 us (99%)
    pallas_call x1, Pallas kernels, device_fn(): pl.pallas_call(functools.partial(kernel, shards, n_heads, hd, scale * mat...  89.3 us
    pallas_call x1, Pallas kernels, device_fn(): pl.pallas_call(functools.partial(hand_out, len(outs)), out_shape=tuple((j...  3.11 us

profile of v4, /device:TPU:0, one launch (start us, length us, event | category | flops | bytes accessed | tf_op | source)
XLA Modules:
  0.0 93.2 jit_solution(7769785681991892302)
XLA Ops:
  0.6 89.3 %attention.1 = (bf16[512,896]{1,0:T(8,128)(2,1)}, bf16[512,896]{1,0:T(8,128)(2,1)}, bf16[7,64,896]{2,1,0:T(8,128)(2,1)}, bf16[64,896]{1,0:T(8,128)(2,1)}, bf16[6...) custom-call(bf16[512,896]{1,0:T(8,128)(2,1)} %x_hbm.1, bf16[512,896]{1,0:T(8,128)(2,1)} %dy_hbm.1, ...), custom_call_target="tpu_custom_call" | custom-call | flops 14797504512 | bytes 16777216 | tf_op jit(solution)/shard_map/attention/pallas_call | solution.py:517
  89.9 3.1 %hand_out.1 = (bf16[512,896]{1,0:T(8,128)(2,1)}, bf16[512,896]{1,0:T(8,128)(2,1)}, bf16[7,64,896]{2,1,0:T(8,128)(2,1)}, bf16[64,896]{1,0:T(8,128)(2,1)}, bf16[64...) custom-call(bf16[512,896]{1,0:T(8,128)(2,1)} %get-tuple-element.18.refs_0_, bf16[512,896]{1,0:T(8,128)(2,1)} %get-tuple-element.19.refs_1_, ...), custom_call_target="tpu_custom_call" | custom-call | bytes 8388608 | tf_op jit(solution)/shard_map/hand_out/pallas_call | solution.py:538

commit v5 on v4

--- a/solution.py
+++ b/solution.py
@@ -17,11 +17,10 @@
 BF16 = jnp.bfloat16
 NT = (((1,), (1,)), ((), ()))
 TN = (((0,), (0,)), ((), ()))
-VMEM = pl.BlockSpec(memory_space=pltpu.VMEM)
 ANY = pl.BlockSpec(memory_space=pl.ANY)
 HBM = pl.BlockSpec(memory_space=pltpu.HBM)
 VMEM_LIMIT = 64 * 1024 * 1024 - 64 * 1024
-N_COPIES = 23
+N_COPIES = 24
 PAD = 16
 BIG = 3.0e38
 
@@ -80,7 +79,7 @@
            y_ref, dx_ref, gq_ref, gk_ref, gv_ref, go_ref,
            x_s, xp, dy_s, dyp, w_own, w_peer,
            q_s, do_s, o_s, og, dq_s, dqg, kvt, k_s, ka, q_n, do_n, acc, m_s, l_s, max_s, s_s, pb, db, dkv, rcv, dkvb, dkvg,
-           y_s, dx_s, dx_f, gq_s, gkv_s, go_s, send, recv, local):
+           y_s, dx_s, dx_f, gq_s, gkv_s, go_s, go_f, send, recv, local):
     rank = lax.axis_index("cp")
     half = lax.axis_index("tp")
     core = rank % 2
@@ -123,11 +122,11 @@
     across = (rank + 2) % shards
     mid = cols // 2
     c_x = [copy(i, x_hbm.at[pl.ds(j * mid, mid)], xp.at[pl.ds(j * mid, mid)], peer) for i, j in ((0, 0), (22, 1))]
-    c_dy = copy(1, dy_hbm, dyp, peer)
+    c_dy = [copy(i, dy_hbm.at[pl.ds(j * mid, mid)], dyp.at[pl.ds(j * mid, mid)], peer) for i, j in ((1, 0), (23, 1))]
     c_w = copy(2, w_own.at[rank], w_peer.at[rank], peer)
     c_relay = [copy(3, w_peer.at[rank], w_peer.at[rank], partner), copy(4, w_peer.at[rank], w_peer.at[rank], at_cp(across)),
                copy(5, w_peer.at[across], w_peer.at[across], partner)]
-    for c in c_x + [c_dy]:
+    for c in c_x + c_dy:
         c.start()
 
     def send_kv(slot):
@@ -156,6 +155,28 @@
     loads[5].wait()
     do_s[0] = dot_nt(weight(w_own, "o"), dy_s[...]).astype(BF16).reshape(n_heads, hd, cols)
     keys_ready(0)
+    part = cols // 2
+    triangle = diag_mask(part)
+
+    def own_diagonal(h, _):
+        s0 = dot(k_s[0, :part], q_s[0, h])
+        s0 = jnp.concatenate([jnp.where(triangle, s0[:, :part], -jnp.inf), s0[:, part:]], axis=1)
+        s1 = jnp.where(triangle, dot(k_s[0, part:], q_s[0, h, :, part:]), -jnp.inf)
+        m0, m1 = jnp.max(s0, axis=0, keepdims=True), jnp.max(s1, axis=0, keepdims=True)
+        m = jnp.concatenate([m0[:, :part], jnp.maximum(m0[:, part:], m1)], axis=1) * c_scale
+        p0, p1 = jnp.exp2(s0 * c_scale - m), jnp.exp2(s1 * c_scale - m[:, part:])
+        zeros = jnp.zeros((8, part), F32)
+        l_s[0, h] = (jnp.sum(p0.reshape(part // 8, 8, cols), axis=0)
+                     + jnp.concatenate([zeros, jnp.sum(p1.reshape(part // 8, 8, part), axis=0)], axis=1))
+        o1 = dot(kvt[0, hd:, part:], p1.astype(BF16))
+        acc[0, h] = dot(kvt[0, hd:, :part], p0.astype(BF16)) + jnp.concatenate([jnp.zeros_like(o1), o1], axis=1)
+        m_s[0, h] = m
+        m_s[1, h] = jnp.full_like(m, -jnp.inf)
+        l_s[1, h] = jnp.zeros((8, cols), F32)
+        acc[1, h] = jnp.zeros((hd, cols), F32)
+        return 0
+
+    lax.fori_loop(0, n_heads, own_diagonal, 0)
     for j, c in enumerate(c_x):
         q = slice(j * mid, (j + 1) * mid)
         c.wait_recv()
@@ -170,8 +191,7 @@
             + shard_units(rank, half, d_near, shards))
     far = shard_units(rank, half, d_far[0], shards) + shard_units(rank, half, d_far[1], shards)
     slots = (half, 1 - half)
-    part = cols // 2
-    triangle = diag_mask(part)
+    near_fwd_units = [(1, 1, half, True)] + near[1:2] + near[3:]
 
     def spans(diag, c):
         return slice(c * part, (c + 1) * part), slice(c * part, cols) if diag else slice(0, cols)
@@ -221,16 +241,11 @@
             max_s[g] = jnp.max(best, axis=0, keepdims=True) * c_scale
 
     def attend_steps(units, base, h, is_near):
-        m = [max_s[0], max_s[1]]
-        if is_near:
-            l = [jnp.zeros((8, cols), F32), jnp.zeros((8, cols), F32)]
-            o = [jnp.zeros((hd, cols), F32), jnp.zeros((hd, cols), F32)]
-        else:
-            old = [m_s[slots[g], h] for g in (0, 1)]
-            m = [jnp.maximum(x, y) for x, y in zip(m, old)]
-            fix = [jnp.exp2(x - y) for x, y in zip(old, m)]
-            l = [l_s[slots[g], h] * fix[g] for g in (0, 1)]
-            o = [acc[slots[g], h] * fix[g] for g in (0, 1)]
+        old = [m_s[slots[g], h] for g in (0, 1)]
+        m = [jnp.maximum(max_s[g], old[g]) for g in (0, 1)]
+        fix = [jnp.exp2(x - y) for x, y in zip(old, m)]
+        l = [l_s[slots[g], h] * fix[g] for g in (0, 1)]
+        o = [acc[slots[g], h] * fix[g] for g in (0, 1)]
         sums = {}
 
         def step(u, c):
@@ -271,7 +286,7 @@
         copy(20, o_s.at[1, h], og.at[h], peer).start()
 
     def near_fwd(h, _):
-        forward(near, 4, h, True, (near, 4, h + 1))
+        forward(near_fwd_units, 4, h, True, (near_fwd_units, 4, h + 1))
         return 0
 
     def far_fwd(h, _):
@@ -285,27 +300,37 @@
         c.wait_recv()
     keys_ready(2 * d_near)
     keys_ready(2 * d_near + 1)
-    for step in score_steps(near, 4, 0, maxes):
+    for step in score_steps(near_fwd_units, 4, 0, maxes):
         step()
-    score_max(near, maxes)
+    score_max(near_fwd_units, maxes)
     lax.fori_loop(0, last, near_fwd, 0)
     for c in (c_kv[0], c_kv[1], c_kv[3], c_kv[4]):
         c.wait_recv()
     for d in d_far:
         keys_ready(2 * d)
         keys_ready(2 * d + 1)
-    forward(near, 4, last, True, (far, 0, 0))
+    forward(near_fwd_units, 4, last, True, (far, 0, 0))
     lax.fori_loop(0, last, far_fwd, 0)
-    c_dy.wait_recv()
-    do_s[1] = dot_nt(weight(w_own, "o"), dyp[...]).astype(BF16).reshape(n_heads, hd, cols)
     forward(far, 0, last, False, None)
     send_o(last)
     dkv[...] = jnp.zeros_like(dkv)
 
-    for h in range(n_heads):
-        for i in (0, 1):
+    def do_ready(i):
+        for h in range(n_heads):
             delta = jnp.sum(do_s[i, h].astype(F32) * o_s[i, h].astype(F32), axis=0, keepdims=True)
             do_n[i, h] = with_columns(do_s[i, h], delta)
+
+    def column_blocks(width):
+        return [slice(start, min(start + 256, width)) for start in range(0, width, 256)]
+
+    do_ready(0)
+    for c in column_blocks(dy_s.shape[1]):
+        go_f[:, c] = dot(o_s[0].reshape(hw, cols), dy_s[:, c])
+    for j, c in enumerate(c_dy):
+        q = slice(j * mid, (j + 1) * mid)
+        c.wait_recv()
+        do_s[1, :, :, q] = dot_nt(weight(w_own, "o"), dyp[q, :]).astype(BF16).reshape(n_heads, hd, mid)
+    do_ready(1)
     lower = lax.broadcasted_iota(jnp.int32, (part, part), 0) >= lax.broadcasted_iota(jnp.int32, (part, part), 1)
 
     def prob_steps(units, bufs, h, u):
@@ -432,13 +457,9 @@
         c.start()
         stores.append(c)
 
-    def weight_grad(out, grads, own, other):
-        for start in range(0, own.shape[1], 256):
-            c = slice(start, min(start + 256, own.shape[1]))
-            g = dot(grads[0].reshape(hw, cols), own[:, c]) + dot(grads[1].reshape(hw, cols), other[:, c])
-            out[:, :, c] = g.astype(BF16).reshape(n_heads, hd, g.shape[1])
-
-    weight_grad(go_s, o_s, dy_s, dyp)
+    for c in column_blocks(dy_s.shape[1]):
+        g = go_f[:, c] + dot(o_s[1].reshape(hw, cols), dyp[:, c])
+        go_s[:, :, c] = g.astype(BF16).reshape(n_heads, hd, g.shape[1])
     leave(go_s, go_ref)
     c_cross.wait_recv()
     c_near.wait_recv()
@@ -449,7 +470,9 @@
         if slot == 1:
             c_last = copy(19, dkvb.at[1], dkvg, peer)
             c_last.start()
-    weight_grad(gq_s, dq_s, x_s, xp)
+    for c in column_blocks(x_s.shape[1]):
+        g = dot(dq_s[0].reshape(hw, cols), x_s[:, c]) + dot(dq_s[1].reshape(hw, cols), xp[:, c])
+        gq_s[:, :, c] = g.astype(BF16).reshape(n_heads, hd, g.shape[1])
     leave(gq_s, gq_ref)
     gkv_s[...] = (dot(dkvb[0], x_s[...]) + dot(dkvb[1], xp[...])).astype(BF16)
     leave(gkv_s.at[:hd], gk_ref)
@@ -458,7 +481,7 @@
     c_o.wait_recv()
     c_relay[0].wait_recv()
     c_relay[2].wait_recv()
-    rows = 128
+    rows = 256
     for i in range(cols // rows):
         blk = slice(i * rows, (i + 1) * rows)
         y = (dot_tn(o_s[0, :, :, blk].reshape(hw, rows), weight(w_own, "o"))
@@ -479,7 +502,7 @@
         dx = dx_f[blk, :] + dot_tn(dkvg[:hd, blk], weight(w_peer, "k")) + dot_tn(dkvg[hd:, blk], weight(w_peer, "v"))
         dx_s[blk, :] = dx.astype(BF16)
     leave(dx_s, dx_ref)
-    for c in c_x + [c_dy, c_o, c_dq, c_last, c_w, c_pair, c_cross, c_near] + c_relay + c_kv:
+    for c in c_x + c_dy + [c_o, c_dq, c_last, c_w, c_pair, c_cross, c_near] + c_relay + c_kv:
         c.wait_send()
     for c in stores:
         c.wait()
@@ -526,9 +549,9 @@
                b(2 * shards, 2 * hd, cols), b(2 * shards, cols, hd), b(2 * shards, 2, hd + PAD, cols),
                b(2, n_heads, cols, hd + PAD), b(2, n_heads, cols, hd + PAD), f(*per_head),
                f(2, n_heads, 1, cols), f(2, n_heads, 8, cols), f(2, 1, cols),
-               f(9, cols, cols), b(5, cols, cols), b(5, cols, cols), f(2 * shards, 2 * hd, cols),
+               f(8, cols, cols), b(5, cols, cols), b(5, cols, cols), f(2 * shards, 2 * hd, cols),
                f(shards - 1, 2, 2 * hd, cols), b(2, 2 * hd, cols), b(2 * hd, cols),
-               b(cols, model), b(cols, model), f(cols, model), b(n_heads, hd, model), b(2 * hd, model), b(n_heads, hd, model),
+               b(cols, model), b(cols, model), f(cols, model), b(n_heads, hd, model), b(2 * hd, model), b(n_heads, hd, model), f(hw, model),
                pltpu.SemaphoreType.DMA((N_COPIES,)), pltpu.SemaphoreType.DMA((N_COPIES,)), pltpu.SemaphoreType.DMA((12,))],
             compiler_params=pltpu.CompilerParams(vmem_limit_bytes=VMEM_LIMIT, collective_id=0, has_side_effects=True),
             cost_estimate=pl.CostEstimate(flops=area * 7 * 2 * hd, bytes_accessed=16 << 20, transcendentals=2 * area),

time: 93.3 us -> 92.1 us (0.987)
  Pallas kernels: 92.4 us -> 91.2 us
    pallas_call x1, Pallas kernels: 89.3 us -> 88.1 us  [device_fn(): pl.pallas_call(functools.partial(kernel, shards, n_heads, hd, scale * mat...]
where the time goes in v5:
time: 92.1 us; the launch traced here: 92 us
  Pallas kernels  91.2 us (99%)
    pallas_call x1, Pallas kernels, device_fn(): pl.pallas_call(functools.partial(kernel, shards, n_heads, hd, scale * mat...  88.1 us
    pallas_call x1, Pallas kernels, device_fn(): pl.pallas_call(functools.partial(hand_out, len(outs)), out_shape=tuple((j...  3.11 us

profile of v5, /device:TPU:0, one launch (start us, length us, event | category | flops | bytes accessed | tf_op | source)
XLA Modules:
  0.0 92.0 jit_solution(12941657683149575818)
XLA Ops:
  0.6 88.1 %attention.1 = (bf16[512,896]{1,0:T(8,128)(2,1)}, bf16[512,896]{1,0:T(8,128)(2,1)}, bf16[7,64,896]{2,1,0:T(8,128)(2,1)}, bf16[64,896]{1,0:T(8,128)(2,1)}, bf16[6...) custom-call(bf16[512,896]{1,0:T(8,128)(2,1)} %x_hbm.1, bf16[512,896]{1,0:T(8,128)(2,1)} %dy_hbm.1, ...), custom_call_target="tpu_custom_call" | custom-call | flops 14797504512 | bytes 16777216 | tf_op jit(solution)/shard_map/attention/pallas_call | solution.py:540
  88.7 3.1 %hand_out.1 = (bf16[512,896]{1,0:T(8,128)(2,1)}, bf16[512,896]{1,0:T(8,128)(2,1)}, bf16[7,64,896]{2,1,0:T(8,128)(2,1)}, bf16[64,896]{1,0:T(8,128)(2,1)}, bf16[64...) custom-call(bf16[512,896]{1,0:T(8,128)(2,1)} %get-tuple-element.18.refs_0_, bf16[512,896]{1,0:T(8,128)(2,1)} %get-tuple-element.19.refs_1_, ...), custom_call_target="tpu_custom_call" | custom-call | bytes 8388608 | tf_op jit(solution)/shard_map/hand_out/pallas_call | solution.py:561

commit v6 on v5

--- a/solution.py
+++ b/solution.py
@@ -187,11 +187,9 @@
         q_s[1, :, :, q] = dot_nt(weight(w_own, "q"), xp[q, :]).astype(BF16).reshape(n_heads, hd, mid)
     keys_ready(1)
 
-    near = ([(half, half, 1, True), (1 - half, half, 0, False), (1 - half, 1 - half, 0, True)]
-            + shard_units(rank, half, d_near, shards))
+    near_rest = [(1, 1, half, True), (1 - half, half, 0, False)] + shard_units(rank, half, d_near, shards)
     far = shard_units(rank, half, d_far[0], shards) + shard_units(rank, half, d_far[1], shards)
     slots = (half, 1 - half)
-    near_fwd_units = [(1, 1, half, True)] + near[1:2] + near[3:]
 
     def spans(diag, c):
         return slice(c * part, (c + 1) * part), slice(c * part, cols) if diag else slice(0, cols)
@@ -286,7 +284,7 @@
         copy(20, o_s.at[1, h], og.at[h], peer).start()
 
     def near_fwd(h, _):
-        forward(near_fwd_units, 4, h, True, (near_fwd_units, 4, h + 1))
+        forward(near_rest, 4, h, True, (near_rest, 4, h + 1))
         return 0
 
     def far_fwd(h, _):
@@ -300,16 +298,16 @@
         c.wait_recv()
     keys_ready(2 * d_near)
     keys_ready(2 * d_near + 1)
-    for step in score_steps(near_fwd_units, 4, 0, maxes):
+    for step in score_steps(near_rest, 4, 0, maxes):
         step()
-    score_max(near_fwd_units, maxes)
+    score_max(near_rest, maxes)
     lax.fori_loop(0, last, near_fwd, 0)
     for c in (c_kv[0], c_kv[1], c_kv[3], c_kv[4]):
         c.wait_recv()
     for d in d_far:
         keys_ready(2 * d)
         keys_ready(2 * d + 1)
-    forward(near_fwd_units, 4, last, True, (far, 0, 0))
+    forward(near_rest, 4, last, True, (far, 0, 0))
     lax.fori_loop(0, last, far_fwd, 0)
     forward(far, 0, last, False, None)
     send_o(last)
@@ -326,11 +324,6 @@
     do_ready(0)
     for c in column_blocks(dy_s.shape[1]):
         go_f[:, c] = dot(o_s[0].reshape(hw, cols), dy_s[:, c])
-    for j, c in enumerate(c_dy):
-        q = slice(j * mid, (j + 1) * mid)
-        c.wait_recv()
-        do_s[1, :, :, q] = dot_nt(weight(w_own, "o"), dyp[q, :]).astype(BF16).reshape(n_heads, hd, mid)
-    do_ready(1)
     lower = lax.broadcasted_iota(jnp.int32, (part, part), 0) >= lax.broadcasted_iota(jnp.int32, (part, part), 1)
 
     def prob_steps(units, bufs, h, u):
@@ -393,15 +386,30 @@
                     ahead[i]()
         return dq
 
-    near_bufs, far_bufs = (0, 1, 2), (3, 4)
+    own = [(0, 0, 1, True)]
+    for step in prob_steps(own, (0,), 0, 0):
+        step()
+    for h in range(n_heads):
+        dq = [jnp.zeros((hd, cols), F32), None]
+        ahead = prob_steps(own, ((h + 1) % 2,), h + 1, 0) if h < last else []
+        interleave(grad_steps(own, (h % 2,), h, 0, dq), ahead)
+        acc[0, h] = dq[0]
+        acc[1, h] = jnp.zeros((hd, cols), F32)
+
+    for j, c in enumerate(c_dy):
+        q = slice(j * mid, (j + 1) * mid)
+        c.wait_recv()
+        do_s[1, :, :, q] = dot_nt(weight(w_own, "o"), dyp[q, :]).astype(BF16).reshape(n_heads, hd, mid)
+    do_ready(1)
+    near_bufs, far_bufs = (0, 1), (2, 3)
 
     def far_bwd(h, nxt):
         dq = backward(far, far_bufs, h, nxt)
         for g in (0, 1):
-            acc[slots[g], h] = dq[g]
+            acc[slots[g], h] += dq[g]
 
     def near_bwd(h, nxt):
-        dq = backward(near, near_bufs, h, nxt)
+        dq = backward(near_rest, near_bufs, h, nxt)
         for g in (0, 1):
             dq_s[slots[g], h] = ((dq[g] + acc[slots[g], h]) * scale).astype(BF16)
         copy(21, dq_s.at[1, h], dqg.at[h], peer).start()
@@ -422,7 +430,7 @@
         return 0
 
     def near_loop(h, _):
-        near_bwd(h, (near, near_bufs, h + 1))
+        near_bwd(h, (near_rest, near_bufs, h + 1))
 
         @pl.when(h == 0)
         def _():
@@ -444,7 +452,7 @@
     for step in prob_steps(far, far_bufs, 0, 0):
         step()
     lax.fori_loop(0, last, far_loop, 0)
-    far_bwd(last, (near, near_bufs, 0))
+    far_bwd(last, (near_rest, near_bufs, 0))
     c_pair.start()
     lax.fori_loop(0, last, near_loop, 0)
     near_bwd(last, None)
@@ -549,7 +557,7 @@
                b(2 * shards, 2 * hd, cols), b(2 * shards, cols, hd), b(2 * shards, 2, hd + PAD, cols),
                b(2, n_heads, cols, hd + PAD), b(2, n_heads, cols, hd + PAD), f(*per_head),
                f(2, n_heads, 1, cols), f(2, n_heads, 8, cols), f(2, 1, cols),
-               f(8, cols, cols), b(5, cols, cols), b(5, cols, cols), f(2 * shards, 2 * hd, cols),
+               f(8, cols, cols), b(4, cols, cols), b(4, cols, cols), f(2 * shards, 2 * hd, cols),
                f(shards - 1, 2, 2 * hd, cols), b(2, 2 * hd, cols), b(2 * hd, cols),
                b(cols, model), b(cols, model), f(cols, model), b(n_heads, hd, model), b(2 * hd, model), b(n_heads, hd, model), f(hw, model),
                pltpu.SemaphoreType.DMA((N_COPIES,)), pltpu.SemaphoreType.DMA((N_COPIES,)), pltpu.SemaphoreType.DMA((12,))],

time: 92.1 us -> 94.4 us (1.025)
  Pallas kernels: 91.2 us -> 93.5 us
    pallas_call x1, Pallas kernels: 88.1 us -> 90.4 us  [device_fn(): pl.pallas_call(functools.partial(kernel, shards, n_heads, hd, scale * mat...]
where the time goes in v6:
time: 94.4 us; the launch traced here: 94.3 us
  Pallas kernels  93.5 us (99%)
    pallas_call x1, Pallas kernels, device_fn(): pl.pallas_call(functools.partial(kernel, shards, n_heads, hd, scale * mat...  90.4 us
    pallas_call x1, Pallas kernels, device_fn(): pl.pallas_call(functools.partial(hand_out, len(outs)), out_shape=tuple((j...  3.11 us

profile of v6, /device:TPU:0, one launch (start us, length us, event | category | flops | bytes accessed | tf_op | source)
XLA Modules:
  0.0 94.3 jit_solution(10236258688166080144)
XLA Ops:
  0.6 90.4 %attention.1 = (bf16[512,896]{1,0:T(8,128)(2,1)}, bf16[512,896]{1,0:T(8,128)(2,1)}, bf16[7,64,896]{2,1,0:T(8,128)(2,1)}, bf16[64,896]{1,0:T(8,128)(2,1)}, bf16[6...) custom-call(bf16[512,896]{1,0:T(8,128)(2,1)} %x_hbm.1, bf16[512,896]{1,0:T(8,128)(2,1)} %dy_hbm.1, ...), custom_call_target="tpu_custom_call" | custom-call | flops 14797504512 | bytes 16777216 | tf_op jit(solution)/shard_map/attention/pallas_call | solution.py:548
  91.0 3.1 %hand_out.1 = (bf16[512,896]{1,0:T(8,128)(2,1)}, bf16[512,896]{1,0:T(8,128)(2,1)}, bf16[7,64,896]{2,1,0:T(8,128)(2,1)}, bf16[64,896]{1,0:T(8,128)(2,1)}, bf16[64...) custom-call(bf16[512,896]{1,0:T(8,128)(2,1)} %get-tuple-element.18.refs_0_, bf16[512,896]{1,0:T(8,128)(2,1)} %get-tuple-element.19.refs_1_, ...), custom_call_target="tpu_custom_call" | custom-call | bytes 8388608 | tf_op jit(solution)/shard_map/hand_out/pallas_call | solution.py:569

commit v7 on v5

--- a/solution.py
+++ b/solution.py
@@ -501,17 +501,20 @@
         blk = slice(i * rows, (i + 1) * rows)
         dx = dx_f[blk, :] + dot_tn(dkvg[:hd, blk], weight(w_peer, "k")) + dot_tn(dkvg[hd:, blk], weight(w_peer, "v"))
         dx_s[blk, :] = dx.astype(BF16)
-    leave(dx_s, dx_ref)
+        leave(dx_s.at[blk], dx_ref.at[blk])
     for c in c_x + c_dy + [c_o, c_dq, c_last, c_w, c_pair, c_cross, c_near] + c_relay + c_kv:
         c.wait_send()
     for c in stores:
         c.wait()
 
 
-def hand_out(n, *refs):
+def hand_out(n, pieces, *refs):
     src, dst, held, sems = refs[:n], refs[n:2 * n], refs[2 * n:3 * n], refs[3 * n]
-    loads = [pltpu.make_async_copy(src[i], held[i], sems.at[0, i]) for i in range(n)]
-    stores = [pltpu.make_async_copy(held[i], dst[i], sems.at[1, i]) for i in range(n)]
+    loads, stores = [], []
+    for j, (i, start, size) in enumerate(pieces):
+        rows = pl.ds(start, size)
+        loads.append(pltpu.make_async_copy(src[i].at[rows], held[i].at[rows], sems.at[0, j]))
+        stores.append(pltpu.make_async_copy(held[i].at[rows], dst[i].at[rows], sems.at[1, j]))
     for c in loads:
         c.start()
     for load, store in zip(loads, stores):
@@ -519,6 +522,14 @@
         store.start()
     for c in stores:
         c.wait()
+
+
+def cut(shapes, most):
+    pieces = []
+    for i, shape in enumerate(shapes):
+        step = max(1, most // (2 * math.prod(shape[1:])))
+        pieces += [(i, start, min(step, shape[0] - start)) for start in range(0, shape[0], step)]
+    return pieces
 
 
 def solution(mesh):
@@ -552,18 +563,19 @@
                f(8, cols, cols), b(5, cols, cols), b(5, cols, cols), f(2 * shards, 2 * hd, cols),
                f(shards - 1, 2, 2 * hd, cols), b(2, 2 * hd, cols), b(2 * hd, cols),
                b(cols, model), b(cols, model), f(cols, model), b(n_heads, hd, model), b(2 * hd, model), b(n_heads, hd, model), f(hw, model),
-               pltpu.SemaphoreType.DMA((N_COPIES,)), pltpu.SemaphoreType.DMA((N_COPIES,)), pltpu.SemaphoreType.DMA((12,))],
+               pltpu.SemaphoreType.DMA((N_COPIES,)), pltpu.SemaphoreType.DMA((N_COPIES,)), pltpu.SemaphoreType.DMA((13,))],
             compiler_params=pltpu.CompilerParams(vmem_limit_bytes=VMEM_LIMIT, collective_id=0, has_side_effects=True),
             cost_estimate=pl.CostEstimate(flops=area * 7 * 2 * hd, bytes_accessed=16 << 20, transcendentals=2 * area),
             name="attention",
         )(x_own, dy_own, wq, wk, wv, wo)
         outs = (y, dx, gq, gk, gv, go)
+        pieces = cut([o.shape for o in outs], 128 * model * 2)
         y, dx, gq, gk, gv, go = pl.pallas_call(
-            functools.partial(hand_out, len(outs)),
+            functools.partial(hand_out, len(outs), pieces),
             out_shape=tuple(jax.ShapeDtypeStruct(o.shape, o.dtype) for o in outs),
             in_specs=[HBM] * len(outs),
             out_specs=(HBM,) * len(outs),
-            scratch_shapes=[pltpu.VMEM(o.shape, o.dtype) for o in outs] + [pltpu.SemaphoreType.DMA((2, len(outs)))],
+            scratch_shapes=[pltpu.VMEM(o.shape, o.dtype) for o in outs] + [pltpu.SemaphoreType.DMA((2, len(pieces)))],
             cost_estimate=pl.CostEstimate(flops=0, bytes_accessed=8 << 20, transcendentals=0),
             name="hand_out",
         )(*outs)

time: 92.1 us -> 92.6 us (level)
  no operation moved by 1% of the time
where the time goes in v7:
time: 92.6 us; the launch traced here: 92.5 us
  Pallas kernels  91.7 us (99%)
    pallas_call x1, Pallas kernels, device_fn(): pl.pallas_call(functools.partial(kernel, shards, n_heads, hd, scale * mat...  87.9 us
    pallas_call x1, Pallas kernels, device_fn(): pl.pallas_call(functools.partial(hand_out, len(outs), pieces), out_shape=...  3.76 us

profile of v7, /device:TPU:0, one launch (start us, length us, event | category | flops | bytes accessed | tf_op | source)
XLA Modules:
  0.0 92.5 jit_solution(12857680962715686471)
XLA Ops:
  0.6 87.9 %attention.1 = (bf16[512,896]{1,0:T(8,128)(2,1)}, bf16[512,896]{1,0:T(8,128)(2,1)}, bf16[7,64,896]{2,1,0:T(8,128)(2,1)}, bf16[64,896]{1,0:T(8,128)(2,1)}, bf16[6...) custom-call(bf16[512,896]{1,0:T(8,128)(2,1)} %x_hbm.1, bf16[512,896]{1,0:T(8,128)(2,1)} %dy_hbm.1, ...), custom_call_target="tpu_custom_call" | custom-call | flops 14797504512 | bytes 16777216 | tf_op jit(solution)/shard_map/attention/pallas_call | solution.py:551
  88.6 3.8 %hand_out.1 = (bf16[512,896]{1,0:T(8,128)(2,1)}, bf16[512,896]{1,0:T(8,128)(2,1)}, bf16[7,64,896]{2,1,0:T(8,128)(2,1)}, bf16[64,896]{1,0:T(8,128)(2,1)}, bf16[64...) custom-call(bf16[512,896]{1,0:T(8,128)(2,1)} %get-tuple-element.18.refs_0_, bf16[512,896]{1,0:T(8,128)(2,1)} %get-tuple-element.19.refs_1_, ...), custom_call_target="tpu_custom_call" | custom-call | bytes 8388608 | tf_op jit(solution)/shard_map/hand_out/pallas_call | solution.py:573

commit v8 on v5

--- a/solution.py
+++ b/solution.py
@@ -217,15 +217,18 @@
                 second_list[j]()
                 j += 1
 
+    def pieces(units):
+        return [(u, c) for u, unit in enumerate(units) for c in ((0, 1) if unit[3] else (None,))]
+
     def score_steps(units, base, h, maxes):
         def step(u, c):
             qi, kt, first, diag = units[u]
-            r, q = spans(diag, c)
+            r, q = spans(diag, c) if diag else (slice(0, cols), slice(0, cols))
             s = masked(dot(k_s[kt, r], q_s[qi, h, :, q]), diag, -jnp.inf)
             s_s[base + u, r, q] = s
-            mx = widen(jnp.max(s.reshape(part // 8, 8, s.shape[1]), axis=0), -jnp.inf)
-            maxes[u] = mx if c == 0 else jnp.maximum(maxes[u], mx)
-        return [functools.partial(step, u, c) for u in range(len(units)) for c in (0, 1)]
+            mx = widen(jnp.max(s.reshape(s.shape[0] // 8, 8, s.shape[1]), axis=0), -jnp.inf)
+            maxes[u] = jnp.maximum(maxes[u], mx) if c == 1 else mx
+        return [functools.partial(step, u, c) for u, c in pieces(units)]
 
     def score_max(units, maxes):
         for g in (0, 1):
@@ -250,11 +253,14 @@
 
         def step(u, c):
             qi, kt, first, diag = units[u]
-            r, q = spans(diag, c)
+            r, q = spans(diag, c) if diag else (slice(0, cols), slice(0, cols))
             p = jnp.exp2(s_s[base + u, r, q] * c_scale - pick(first, m)[:, q])
-            l_u = widen(jnp.sum(p.reshape(part // 8, 8, p.shape[1]), axis=0), 0.0)
+            l_u = widen(jnp.sum(p.reshape(p.shape[0] // 8, 8, p.shape[1]), axis=0), 0.0)
             o_u = widen(dot(kvt[kt, hd:, r], p.astype(BF16)), 0.0)
-            if c == 0:
+            if c is None:
+                add_to(l, first, l_u)
+                add_to(o, first, o_u)
+            elif c == 0:
                 sums[u] = (l_u, o_u)
             else:
                 add_to(l, first, sums[u][0] + l_u)
@@ -271,7 +277,7 @@
                     o_s[slots[g], h] = (o[g] / l_row).astype(BF16)
                     q_n[slots[g], h] = with_columns(q_s[slots[g], h], (m[g] + jnp.log2(l_row)) * (1.0 / c_scale))
 
-        return [functools.partial(step, u, c) for u in range(len(units)) for c in (0, 1)], finish
+        return [functools.partial(step, u, c) for u, c in pieces(units)], finish
 
     def forward(units, base, h, is_near, nxt):
         steps, finish = attend_steps(units, base, h, is_near)
@@ -461,6 +467,13 @@
         g = go_f[:, c] + dot(o_s[1].reshape(hw, cols), dyp[:, c])
         go_s[:, :, c] = g.astype(BF16).reshape(n_heads, hd, g.shape[1])
     leave(go_s, go_ref)
+
+    def query_weights(blocks):
+        for c in blocks:
+            g = dot(dq_s[0].reshape(hw, cols), x_s[:, c]) + dot(dq_s[1].reshape(hw, cols), xp[:, c])
+            gq_s[:, :, c] = g.astype(BF16).reshape(n_heads, hd, g.shape[1])
+
+    query_weights(column_blocks(x_s.shape[1])[:2])
     c_cross.wait_recv()
     c_near.wait_recv()
     for slot in (1, 0):
@@ -470,9 +483,7 @@
         if slot == 1:
             c_last = copy(19, dkvb.at[1], dkvg, peer)
             c_last.start()
-    for c in column_blocks(x_s.shape[1]):
-        g = dot(dq_s[0].reshape(hw, cols), x_s[:, c]) + dot(dq_s[1].reshape(hw, cols), xp[:, c])
-        gq_s[:, :, c] = g.astype(BF16).reshape(n_heads, hd, g.shape[1])
+    query_weights(column_blocks(x_s.shape[1])[2:])
     leave(gq_s, gq_ref)
     gkv_s[...] = (dot(dkvb[0], x_s[...]) + dot(dkvb[1], xp[...])).astype(BF16)
     leave(gkv_s.at[:hd], gk_ref)
@@ -501,7 +512,7 @@
         blk = slice(i * rows, (i + 1) * rows)
         dx = dx_f[blk, :] + dot_tn(dkvg[:hd, blk], weight(w_peer, "k")) + dot_tn(dkvg[hd:, blk], weight(w_peer, "v"))
         dx_s[blk, :] = dx.astype(BF16)
-    leave(dx_s, dx_ref)
+        leave(dx_s.at[blk], dx_ref.at[blk])
     for c in c_x + c_dy + [c_o, c_dq, c_last, c_w, c_pair, c_cross, c_near] + c_relay + c_kv:
         c.wait_send()
     for c in stores:
@@ -552,7 +563,7 @@
                f(8, cols, cols), b(5, cols, cols), b(5, cols, cols), f(2 * shards, 2 * hd, cols),
                f(shards - 1, 2, 2 * hd, cols), b(2, 2 * hd, cols), b(2 * hd, cols),
                b(cols, model), b(cols, model), f(cols, model), b(n_heads, hd, model), b(2 * hd, model), b(n_heads, hd, model), f(hw, model),
-               pltpu.SemaphoreType.DMA((N_COPIES,)), pltpu.SemaphoreType.DMA((N_COPIES,)), pltpu.SemaphoreType.DMA((12,))],
+               pltpu.SemaphoreType.DMA((N_COPIES,)), pltpu.SemaphoreType.DMA((N_COPIES,)), pltpu.SemaphoreType.DMA((13,))],
             compiler_params=pltpu.CompilerParams(vmem_limit_bytes=VMEM_LIMIT, collective_id=0, has_side_effects=True),
             cost_estimate=pl.CostEstimate(flops=area * 7 * 2 * hd, bytes_accessed=16 << 20, transcendentals=2 * area),
             name="attention",

time: 92.1 us -> 92 us (level)
  no operation moved by 1% of the time
where the time goes in v8:
time: 92 us; the launch traced here: 91.9 us
  Pallas kernels  91.1 us (99%)
    pallas_call x1, Pallas kernels, device_fn(): pl.pallas_call(functools.partial(kernel, shards, n_heads, hd, scale * mat...  87.9 us
    pallas_call x1, Pallas kernels, device_fn(): pl.pallas_call(functools.partial(hand_out, len(outs)), out_shape=tuple((j...  3.11 us

profile of v8, /device:TPU:0, one launch (start us, length us, event | category | flops | bytes accessed | tf_op | source)
XLA Modules:
  0.0 91.9 jit_solution(3636771244379522698)
XLA Ops:
  0.6 87.9 %attention.1 = (bf16[512,896]{1,0:T(8,128)(2,1)}, bf16[512,896]{1,0:T(8,128)(2,1)}, bf16[7,64,896]{2,1,0:T(8,128)(2,1)}, bf16[64,896]{1,0:T(8,128)(2,1)}, bf16[6...) custom-call(bf16[512,896]{1,0:T(8,128)(2,1)} %x_hbm.1, bf16[512,896]{1,0:T(8,128)(2,1)} %dy_hbm.1, ...), custom_call_target="tpu_custom_call" | custom-call | flops 14797504512 | bytes 16777216 | tf_op jit(solution)/shard_map/attention/pallas_call | solution.py:551
  88.6 3.1 %hand_out.1 = (bf16[512,896]{1,0:T(8,128)(2,1)}, bf16[512,896]{1,0:T(8,128)(2,1)}, bf16[7,64,896]{2,1,0:T(8,128)(2,1)}, bf16[64,896]{1,0:T(8,128)(2,1)}, bf16[64...) custom-call(bf16[512,896]{1,0:T(8,128)(2,1)} %get-tuple-element.18.refs_0_, bf16[512,896]{1,0:T(8,128)(2,1)} %get-tuple-element.19.refs_1_, ...), custom_call_target="tpu_custom_call" | custom-call | bytes 8388608 | tf_op jit(solution)/shard_map/hand_out/pallas_call | solution.py:572

commit v9 on v8

--- a/solution.py
+++ b/solution.py
@@ -177,6 +177,11 @@
         return 0
 
     lax.fori_loop(0, n_heads, own_diagonal, 0)
+    dkv[...] = jnp.zeros_like(dkv)
+    for c in c_kv:
+        c.wait_recv()
+    for d in (d_near,) + d_far:
+        keys_ready(2 * d)
     for j, c in enumerate(c_x):
         q = slice(j * mid, (j + 1) * mid)
         c.wait_recv()
@@ -302,24 +307,20 @@
 
     last = n_heads - 1
     maxes = {}
-    for c in (c_kv[2], c_kv[5]):
-        c.wait_recv()
-    keys_ready(2 * d_near)
+    c_kv[5].wait_recv()
     keys_ready(2 * d_near + 1)
     for step in score_steps(near_fwd_units, 4, 0, maxes):
         step()
     score_max(near_fwd_units, maxes)
     lax.fori_loop(0, last, near_fwd, 0)
-    for c in (c_kv[0], c_kv[1], c_kv[3], c_kv[4]):
+    for c in c_kv[3:5]:
         c.wait_recv()
     for d in d_far:
-        keys_ready(2 * d)
         keys_ready(2 * d + 1)
     forward(near_fwd_units, 4, last, True, (far, 0, 0))
     lax.fori_loop(0, last, far_fwd, 0)
     forward(far, 0, last, False, None)
     send_o(last)
-    dkv[...] = jnp.zeros_like(dkv)
 
     def do_ready(i):
         for h in range(n_heads):

time: 92 us -> 92 us (level)
  no operation moved by 1% of the time
where the time goes in v9:
time: 92 us; the launch traced here: 91.9 us
  Pallas kernels  91 us (99%)
    pallas_call x1, Pallas kernels, device_fn(): pl.pallas_call(functools.partial(kernel, shards, n_heads, hd, scale * mat...  87.9 us
    pallas_call x1, Pallas kernels, device_fn(): pl.pallas_call(functools.partial(hand_out, len(outs)), out_shape=tuple((j...  3.11 us

profile of v9, /device:TPU:0, one launch (start us, length us, event | category | flops | bytes accessed | tf_op | source)
XLA Modules:
  0.0 91.9 jit_solution(9138445628376885559)
XLA Ops:
  0.6 87.9 %attention.1 = (bf16[512,896]{1,0:T(8,128)(2,1)}, bf16[512,896]{1,0:T(8,128)(2,1)}, bf16[7,64,896]{2,1,0:T(8,128)(2,1)}, bf16[64,896]{1,0:T(8,128)(2,1)}, bf16[6...) custom-call(bf16[512,896]{1,0:T(8,128)(2,1)} %x_hbm.1, bf16[512,896]{1,0:T(8,128)(2,1)} %dy_hbm.1, ...), custom_call_target="tpu_custom_call" | custom-call | flops 14797504512 | bytes 16777216 | tf_op jit(solution)/shard_map/attention/pallas_call | solution.py:552
  88.6 3.1 %hand_out.1 = (bf16[512,896]{1,0:T(8,128)(2,1)}, bf16[512,896]{1,0:T(8,128)(2,1)}, bf16[7,64,896]{2,1,0:T(8,128)(2,1)}, bf16[64,896]{1,0:T(8,128)(2,1)}, bf16[64...) custom-call(bf16[512,896]{1,0:T(8,128)(2,1)} %get-tuple-element.18.refs_0_, bf16[512,896]{1,0:T(8,128)(2,1)} %get-tuple-element.19.refs_1_, ...), custom_call_target="tpu_custom_call" | custom-call | bytes 8388608 | tf_op jit(solution)/shard_map/hand_out/pallas_call | solution.py:573
